TPU v7x, 32 devices: a whole 2x2x4 slice. The times are simulated.
32 devices in a mesh: gx: 8 (over z, y), gy: 4 (over x, core).
Axes of the slice: x: 2, y: 2, z: 4, core: 2. Of those that a mesh axis runs over, the one named last changes fastest.
Arguments:
- tokens: bfloat16 [256, 8192], P('gy', 'gx'), may hold values from -6 to 6
- target: bfloat16 [256, 8192], P('gy', 'gx'), may hold values from -6 to 6
- w_gate: bfloat16 [8192, 14336], P('gx', 'gy'), may hold values from -0.0625 to 0.0625
- w_up: bfloat16 [8192, 14336], P('gx', 'gy'), may hold values from -0.0625 to 0.0625
- w_down: bfloat16 [14336, 8192], P('gy', 'gx'), may hold values from -0.046875 to 0.046875
- t_gate: bfloat16 [8192, 14336], P('gx', 'gy'), may hold values from -0.0625 to 0.0625
- t_up: bfloat16 [8192, 14336], P('gx', 'gy'), may hold values from -0.0625 to 0.0625
- t_down: bfloat16 [14336, 8192], P('gy', 'gx'), may hold values from -0.046875 to 0.046875
Outputs:
- hvp_gate: bfloat16 [8192, 14336], P('gx', 'gy')
- hvp_up: bfloat16 [8192, 14336], P('gx', 'gy')
- hvp_down: bfloat16 [14336, 8192], P('gy', 'gx')
All inputs are finite; a program needn't handle non-finite values.
Results may differ from a plain program's by a relative error of at most 0.0074.
Values may be sent and summed in bfloat16 or wider, within the bound.
A program may use at most 192 MiB of HBM per device.

v0:
```python
import functools
import math

import jax
import jax.numpy as jnp
from jax import lax
from jax.experimental import pallas as pl
from jax.experimental.pallas import tpu as pltpu
from jax.sharding import PartitionSpec as P

TOKENS = 256


def silu_parts(gate):
    sig = jax.nn.sigmoid(gate)
    first = sig * (1.0 + gate * (1.0 - sig))
    second = sig * (1.0 - sig) * (2.0 + gate * (1.0 - 2.0 * sig))
    return (gate * sig, first, second)


def matmul(left, right):
    return jnp.dot(left, right, preferred_element_type=jnp.float32)


def lead_dot(left, right):
    return lax.dot_general(
        left, right, (((0,), (0,)), ((), ())), preferred_element_type=jnp.float32
    )


def tail_dot(left, right):
    return lax.dot_general(
        left, right, (((1,), (1,)), ((), ())), preferred_element_type=jnp.float32
    )


def gather_kernel(axis, count, arrays, *refs):
    blocks, fulls = refs[:arrays], refs[arrays : 2 * arrays]
    own_sem, send, recv = refs[2 * arrays :]
    pairs = count // 2
    me = lax.axis_index(axis)
    side = lax.rem(me, 2)
    pair = lax.div(me, 2)
    partner = me + 1 - 2 * side
    peers = [lax.rem(pair + step, pairs) * 2 + side for step in range(1, pairs)]
    sources = [lax.rem(pair + pairs - step, pairs) * 2 + side for step in range(1, pairs)]
    rows = blocks[0].shape[0]

    def place(full, index):
        return full.at[pl.ds(pl.multiple_of(index * rows, rows), rows)]

    barrier = pltpu.get_barrier_semaphore()
    for peer in [partner, *peers]:
        pl.semaphore_signal(
            barrier, inc=1, device_id={axis: peer}, device_id_type=pl.DeviceIdType.MESH
        )
    pl.semaphore_wait(barrier, pairs)

    def remote(src, full, index, peer, slot):
        return pltpu.make_async_remote_copy(
            src_ref=src,
            dst_ref=place(full, index),
            send_sem=send.at[slot],
            recv_sem=recv.at[slot],
            device_id={axis: peer},
            device_id_type=pl.DeviceIdType.MESH,
        )

    slots = 2 * pairs - 1
    direct, final, own = {}, [], []
    for i in range(arrays):
        for step, peer in enumerate(peers):
            direct[i, step] = remote(blocks[i], fulls[i], me, peer, i * slots + step)
            direct[i, step].start()
        copy = remote(blocks[i], fulls[i], me, partner, i * slots + pairs - 1)
        copy.start()
        final.append(copy)
        own.append(pltpu.make_async_copy(blocks[i], place(fulls[i], me), own_sem.at[i]))
        own[-1].start()
    for i in range(arrays):
        for step, source in enumerate(sources):
            direct[i, step].wait_recv()
            copy = remote(
                place(fulls[i], source), fulls[i], source, partner, i * slots + pairs + step
            )
            copy.start()
            final.append(copy)
    for copy in direct.values():
        copy.wait_send()
    for copy in final + own:
        copy.wait()


def gather(blocks, axis, collective_id):
    count = lax.axis_size(axis)
    arrays = len(blocks)
    slots = arrays * (count - 1)
    sent = sum(block.size * 2 * (count - 1) for block in blocks)
    return pl.pallas_call(
        functools.partial(gather_kernel, axis, count, arrays),
        out_shape=[
            jax.ShapeDtypeStruct((count * block.shape[0], block.shape[1]), block.dtype)
            for block in blocks
        ],
        in_specs=[pl.BlockSpec(memory_space=pltpu.VMEM)] * arrays,
        out_specs=[pl.BlockSpec(memory_space=pl.ANY)] * arrays,
        scratch_shapes=[
            pltpu.SemaphoreType.DMA((arrays,)),
            pltpu.SemaphoreType.DMA((slots,)),
            pltpu.SemaphoreType.DMA((slots,)),
        ],
        compiler_params=pltpu.CompilerParams(
            collective_id=collective_id, has_side_effects=True
        ),
        cost_estimate=pl.CostEstimate(
            flops=0, bytes_accessed=16 * sent, transcendentals=0
        ),
    )(*blocks)


def products_kernel(turned, gate, upper, out_gate, out_up):
    out_gate[...] = matmul(turned[...], gate[...]).astype(out_gate.dtype)
    out_up[...] = matmul(turned[...], upper[...]).astype(out_up.dtype)


def weight_products(turned, gate, upper):
    rows, depth = turned.shape
    width = gate.shape[1]
    tile = next(size for size in (512, 256, 128) if width % size == 0)
    return pl.pallas_call(
        products_kernel,
        grid=(width // tile,),
        in_specs=[
            pl.BlockSpec((rows, depth), lambda i: (0, 0)),
            pl.BlockSpec((depth, tile), lambda i: (0, i)),
            pl.BlockSpec((depth, tile), lambda i: (0, i)),
        ],
        out_specs=[pl.BlockSpec((rows, tile), lambda i: (0, i))] * 2,
        out_shape=[jax.ShapeDtypeStruct((rows, width), jnp.bfloat16)] * 2,
        cost_estimate=pl.CostEstimate(
            flops=4 * rows * depth * width,
            bytes_accessed=4 * (rows + depth) * width,
            transcendentals=0,
        ),
    )(turned, gate, upper)


def scatter_kernel(axis, count, arrays, *refs):
    parts, outs = refs[:arrays], refs[arrays : 2 * arrays]
    landed, held, got, send1, recv1, send2, recv2 = refs[2 * arrays :]
    pairs = count // 2
    me = lax.axis_index(axis)
    side = lax.rem(me, 2)
    pair = lax.div(me, 2)
    partner = me + 1 - 2 * side
    targets = [lax.rem(pair + step, pairs) * 2 for step in range(1, pairs)]
    peers = [target + side for target in targets]

    barrier = pltpu.get_barrier_semaphore()
    for peer in [partner, *peers]:
        pl.semaphore_signal(
            barrier, inc=1, device_id={axis: peer}, device_id_type=pl.DeviceIdType.MESH
        )
    pl.semaphore_wait(barrier, pairs)

    first = {}
    for i in range(arrays):
        for k, target in enumerate([*targets, pair * 2]):
            first[i, k] = pltpu.make_async_remote_copy(
                src_ref=parts[i].at[target + 1 - side],
                dst_ref=landed.at[i, k],
                send_sem=send1.at[i * pairs + k],
                recv_sem=recv1.at[i * pairs + k],
                device_id={axis: partner},
                device_id_type=pl.DeviceIdType.MESH,
            )
            first[i, k].start()
    second = {}
    for i in range(arrays):
        for k, target in enumerate([*targets, pair * 2]):
            first[i, k].wait_recv()
            term = parts[i][target + side].astype(jnp.float32) + landed[i, k].astype(jnp.float32)
            if k == pairs - 1:
                outs[i][...] = term
                continue
            held[i, k] = term.astype(held.dtype)
            second[i, k] = pltpu.make_async_remote_copy(
                src_ref=held.at[i, k],
                dst_ref=got.at[i, k],
                send_sem=send2.at[i * pairs + k],
                recv_sem=recv2.at[i * pairs + k],
                device_id={axis: peers[k]},
                device_id_type=pl.DeviceIdType.MESH,
            )
            second[i, k].start()
    for i in range(arrays):
        for k in range(pairs - 1):
            second[i, k].wait_recv()
            outs[i][...] += got[i, k].astype(jnp.float32)
    for copy in [*first.values(), *second.values()]:
        copy.wait_send()


def scatter_sum(partials, axis, collective_id):
    count = lax.axis_size(axis)
    pairs = count // 2
    arrays = len(partials)
    rows, columns = partials[0].shape[0] // count, partials[0].shape[1]
    parts = [p.astype(jnp.bfloat16).reshape(count, rows, columns) for p in partials]
    sent = 2 * rows * columns * arrays * (count - 1)
    return pl.pallas_call(
        functools.partial(scatter_kernel, axis, count, arrays),
        out_shape=[jax.ShapeDtypeStruct((rows, columns), jnp.float32)] * arrays,
        in_specs=[pl.BlockSpec(memory_space=pltpu.VMEM)] * arrays,
        out_specs=[pl.BlockSpec(memory_space=pltpu.VMEM)] * arrays,
        scratch_shapes=[
            pltpu.VMEM((arrays, pairs, rows, columns), jnp.bfloat16),
            pltpu.VMEM((arrays, max(pairs - 1, 1), rows, columns), jnp.bfloat16),
            pltpu.VMEM((arrays, max(pairs - 1, 1), rows, columns), jnp.bfloat16),
            *[pltpu.SemaphoreType.DMA((arrays * pairs,))] * 4,
        ],
        compiler_params=pltpu.CompilerParams(
            collective_id=collective_id, has_side_effects=True
        ),
        cost_estimate=pl.CostEstimate(flops=0, bytes_accessed=16 * sent, transcendentals=0),
    )(*parts)


def body(tokens, target, w_gate, w_up, w_down, t_gate, t_up, t_down):
    scale = 1.0 / math.sqrt(TOKENS)
    (xfull,) = gather([tokens], "gy", 0)
    rows = xfull
    gate, upper, gate_dot, upper_dot = scatter_sum(
        [matmul(rows, w) for w in (w_gate, w_up, t_gate, t_up)], "gx", 4
    )
    silu_val, first, second = silu_parts(gate)
    hidden = (silu_val * upper).astype(jnp.bfloat16)
    hidden_dot = (first * gate_dot * upper + silu_val * upper_dot).astype(jnp.bfloat16)
    hid_full, hid_dot_full = gather([hidden, hidden_dot], "gx", 1)
    rows = hid_full
    rows_dot = hid_dot_full
    output = matmul(rows, w_down)
    output_dot = matmul(rows_dot, w_down) + matmul(rows, t_down)
    output, output_dot = scatter_sum([output, output_dot], "gy", 6)
    grad = ((output - target.astype(jnp.float32)) * scale).astype(jnp.bfloat16)
    grad_dot = (output_dot * scale).astype(jnp.bfloat16)
    grad_full, grad_dot_full = gather([grad, grad_dot], "gy", 2)
    hvp_down = (lead_dot(hid_dot_full, grad_full) + lead_dot(hid_full, grad_dot_full)).astype(
        jnp.bfloat16
    )
    rows = grad_full
    rows_dot = grad_dot_full
    back = tail_dot(rows, w_down)
    back_dot = tail_dot(rows_dot, w_down) + tail_dot(rows, t_down)
    back, back_dot = scatter_sum([back, back_dot], "gx", 5)
    gate_in = (
        back_dot * upper * first + back * upper_dot * first + back * upper * second * gate_dot
    ).astype(jnp.bfloat16)
    upper_in = (back_dot * silu_val + back * first * gate_dot).astype(jnp.bfloat16)
    gate_full, upper_full = gather([gate_in, upper_in], "gx", 3)
    hvp_gate, hvp_up = weight_products(lax.optimization_barrier(xfull.T), gate_full, upper_full)
    return (hvp_gate, hvp_up, hvp_down)


def solution(mesh):
    return jax.shard_map(
        body,
        mesh=mesh,
        in_specs=(
            P("gy", "gx"),
            P("gy", "gx"),
            P("gx", "gy"),
            P("gx", "gy"),
            P("gy", "gx"),
            P("gx", "gy"),
            P("gx", "gy"),
            P("gy", "gx"),
        ),
        out_specs=(P("gx", "gy"), P("gx", "gy"), P("gy", "gx")),
        check_vma=False,
    )
```

profile of v0, /device:TPU:0, one launch (start us, length us, event | category | flops | bytes accessed | tf_op | source)
XLA Modules:
  0.0 361.4 jit_solution(17400156778490045076)
XLA Ops:
  0.6 9.5 %shard_map.103 = bf16[256,1024]{1,0:T(8,128)(2,1)} custom-call(bf16[64,1024]{1,0:T(8,128)(2,1)} %refs_0_.1), custom_call_target="tpu_custom_call" | custom-call | bytes 6291456 | tf_op jit(solution)/shard_map/pallas_call | solution.py:99
  10.2 0.0 copy-start.1
  10.2 0.0 copy-start.10
  10.2 0.0 slice-start
  10.2 6.7 %convolution_convert_fusion.4 = bf16[256,3584]{1,0:T(8,128)(2,1)} fusion(bf16[256,1024]{1,0:T(8,128)(2,1)} %shard_map.103, bf16[1024,3584]{1,0:T(8,128)(2,1)} %param.10), kind=kOutput, calls=%fused_computation.6 | convolution fusion | flops 1879965696 | bytes 9699328 | tf_op jit(solution)/shard_map/dot_general | solution.py:22
  16.9 0.0 copy-done.1
  16.9 0.0 copy-done.10
  16.9 0.0 slice-start.1
  16.9 0.0 slice-start.2
  16.9 3.3 convolution_convert_fusion.3
  20.2 0.0 slice-start.3
  20.2 0.0 slice-done
  20.2 0.0 slice-done.1
  20.2 3.3 convolution_convert_fusion.2
  23.5 0.0 slice-done.2
  23.5 0.0 slice-done.3
  23.5 3.3 convolution_convert_fusion.1
  26.9 95.7 %shard_map.104 = (f32[32,3584]{1,0:T(8,128)}, f32[32,3584]{1,0:T(8,128)}, f32[32,3584]{1,0:T(8,128)}, f32[32,3584]{1,0:T(8,128)}) custom-call(bf16[8,32,3584]{2,1,0:T(8,128)(2,1)} %bitcast.33, bf16[8,32,3584]{2,1,0:T(8,128)(2,1)} %bitcast.34, bf16[8,32,3584]{2,1,0:T(8,128)(2,1)} %bitcast.35, bf16[8,32,3584]{2,1,0:T(8,128)(2,1)} %bitcast.36), custom_call_target="tpu_custom_call" | custom-call | bytes 102760448 | tf_op jit(solution)/shard_map/pallas_call | solution.py:211
  122.5 2.4 add_convert_fusion.2
  125.0 50.5 %shard_map.105 = (bf16[256,3584]{1,0:T(8,128)(2,1)}, bf16[256,3584]{1,0:T(8,128)(2,1)}) custom-call(bf16[32,3584]{1,0:T(8,128)(2,1)} %get-tuple-element.38.refs_0_, bf16[32,3584]{1,0:T(8,128)(2,1)} %get-tuple-element.37.refs_1_), custom_call_target="tpu_custom_call" | custom-call | bytes 51380224 | tf_op jit(solution)/shard_map/pallas_call | solution.py:99
  175.5 0.0 copy-start.2
  175.5 0.0 slice-start.4
  175.5 5.8 %fusion.10 = f32[256,1024]{1,0:T(8,128)S(1)} fusion(bf16[256,3584]{1,0:T(8,128)(2,1)} %get-tuple-element.24, bf16[3584,1024]{1,0:T(8,128)(2,1)} %param.12), kind=kOutput, calls=%fused_computation.27 | convolution fusion | flops 1879048192 | bytes 10223616 | tf_op jit(solution)/shard_map/dot_general | solution.py:22
  181.4 0.0 copy-done.2
  181.4 0.0 slice-start.5
  181.4 6.3 %fusion.1 = bf16[256,1024]{1,0:T(8,128)(2,1)} fusion(f32[256,1024]{1,0:T(8,128)S(1)} %fusion.10, bf16[256,3584]{1,0:T(8,128)(2,1)S(1)} %copy-done.2, bf16[3584,1024]{1,0:T(8,128)(2,1)} %param.15), kind=kOutput, calls=%fused_computation.9 | convolution fusion | flops 1879572480 | bytes 10747904 | tf_op jit(solution)/shard_map/dot_general | solution.py:22
  187.7 0.0 slice-done.4
  187.7 0.0 slice-done.5
  187.7 0.0 copy-start.9
  187.7 0.0 copy-start
  187.7 3.0 convolution_convert_fusion.5
  190.7 11.5 %shard_map.106 = (f32[64,1024]{1,0:T(8,128)}, f32[64,1024]{1,0:T(8,128)}) custom-call(bf16[4,64,1024]{2,1,0:T(8,128)(2,1)} %bitcast.41, bf16[4,64,1024]{2,1,0:T(8,128)(2,1)} %bitcast.40), custom_call_target="tpu_custom_call" | custom-call | bytes 12582912 | tf_op jit(solution)/shard_map/pallas_call | solution.py:211
  202.3 0.0 copy-done.9
  202.3 1.8 multiply_convert_fusion.1
  204.0 10.9 %shard_map.107 = (bf16[256,1024]{1,0:T(8,128)(2,1)}, bf16[256,1024]{1,0:T(8,128)(2,1)}) custom-call(bf16[64,1024]{1,0:T(8,128)(2,1)} %get-tuple-element.40.refs_0_, bf16[64,1024]{1,0:T(8,128)(2,1)} %get-tuple-element.39.refs_1_), custom_call_target="tpu_custom_call" | custom-call | bytes 12582912 | tf_op jit(solution)/shard_map/pallas_call | solution.py:99
  214.9 0.0 copy-done
  214.9 0.0 copy-start.8
  214.9 3.2 fusion.12
  218.1 0.0 copy-done.8
  218.2 6.7 %add_convert_fusion = bf16[3584,1024]{1,0:T(8,128)(2,1)} fusion(f32[3584,1024]{1,0:T(8,128)S(1)} %fusion.12, bf16[256,3584]{1,0:T(8,128)(2,1)} %get-tuple-element.23, bf16[256,1024]{1,0:T(8,128)(2,1)S(1)} %copy-done.8), kind=kOutput, calls=%fused_computation | convolution fusion | flops 1886388224 | bytes 24379392 | tf_op jit(solution)/shard_map/dot_general | solution.py:26
  224.9 0.0 copy-start.7
  224.9 0.0 slice-start.6
  224.9 5.4 %fusion.11 = f32[256,3584]{1,0:T(8,128)S(1)} fusion(bf16[256,1024]{1,0:T(8,128)(2,1)S(1)} %copy-done.8, bf16[3584,1024]{1,0:T(8,128)(2,1)} %param.12), kind=kOutput, calls=%fused_computation.28 | convolution fusion | flops 1879048192 | bytes 11534336 | tf_op jit(solution)/shard_map/dot_general | solution.py:32
  230.3 0.0 copy-done.7
  230.3 0.0 slice-start.7
  230.3 6.6 %fusion = bf16[256,3584]{1,0:T(8,128)(2,1)} fusion(f32[256,3584]{1,0:T(8,128)S(1)} %fusion.11, bf16[256,1024]{1,0:T(8,128)(2,1)S(1)} %copy-done.7, bf16[3584,1024]{1,0:T(8,128)(2,1)} %param.15), kind=kOutput, calls=%fused_computation.7 | convolution fusion | flops 1880883200 | bytes 13369344 | tf_op jit(solution)/shard_map/dot_general | solution.py:32
  236.9 0.0 slice-done.6
  236.9 0.0 slice-done.7
  237.0 0.0 copy-start.3
  237.0 0.0 copy-start.4
  237.0 0.0 copy-start.5
  237.0 0.0 copy-start.6
  237.0 3.3 convolution_convert_fusion
  240.3 57.8 %shard_map.108 = (f32[32,3584]{1,0:T(8,128)}, f32[32,3584]{1,0:T(8,128)}) custom-call(bf16[8,32,3584]{2,1,0:T(8,128)(2,1)} %bitcast.38, bf16[8,32,3584]{2,1,0:T(8,128)(2,1)} %bitcast.37), custom_call_target="tpu_custom_call" | custom-call | bytes 51380224 | tf_op jit(solution)/shard_map/pallas_call | solution.py:211
  298.1 0.0 copy-done.3
  298.1 0.0 copy-done.4
  298.1 0.0 copy-done.5
  298.2 0.0 copy-done.6
  298.2 2.3 add_convert_fusion.1
  300.5 50.4 %shard_map.109 = (bf16[256,3584]{1,0:T(8,128)(2,1)}, bf16[256,3584]{1,0:T(8,128)(2,1)}) custom-call(bf16[32,3584]{1,0:T(8,128)(2,1)} %get-tuple-element.36.refs_0_, bf16[32,3584]{1,0:T(8,128)(2,1)} %get-tuple-element.35.refs_1_), custom_call_target="tpu_custom_call" | custom-call | bytes 51380224 | tf_op jit(solution)/shard_map/pallas_call | solution.py:99
  350.9 1.0 copy.11
  351.9 9.4 %shard_map.110 = (bf16[1024,3584]{1,0:T(8,128)(2,1)}, bf16[1024,3584]{1,0:T(8,128)(2,1)}) custom-call(bf16[1024,256]{1,0:T(8,128)(2,1)} %bitcast.39, bf16[256,3584]{1,0:T(8,128)(2,1)} %get-tuple-element.31.gate, bf16[256,3584]{1,0:T(8,128)(2,1)} %get-tuple-element.32.upper), custom_call_target="tpu_custom_call" | custom-call | flops 3758096384 | bytes 18350080 | tf_op jit(solution)/shard_map/pallas_call | solution.py:130
  (4 shorter events, 0.0 us)
Async XLA Ops:
  10.2 6.7 %copy-start.1 = (bf16[256,1024]{1,0:T(8,128)(2,1)S(1)}, bf16[256,1024]{1,0:T(8,128)(2,1)}, u32[]{:S(2)}) copy-start(bf16[256,1024]{1,0:T(8,128)(2,1)} %shard_map.103) | copy-start | bytes 1572868
  10.2 6.7 %copy-start.10 = (bf16[1024,3584]{1,0:T(8,128)(2,1)S(1)}, bf16[1024,3584]{1,0:T(8,128)(2,1)}, u32[]{:S(2)}) copy-start(bf16[1024,3584]{1,0:T(8,128)(2,1)} %param.11) | copy-start | bytes 22020100
  10.2 10.0 %slice-start = ((s8[7340032]{0:T(1024)(128)(4,1)}), s8[4194304]{0:T(1024)(128)(4,1)S(1)}, s32[]{:S(2)}) async-start(s8[7340032]{0:T(1024)(128)(4,1)} %bitcast.42), calls=%async_computation | async-start | bytes 8388608
  16.9 3.3 slice-start.1
  16.9 6.6 %slice-start.2 = ((s8[7340032]{0:T(1024)(128)(4,1)}), s8[4194304]{0:T(1024)(128)(4,1)S(1)}, s32[]{:S(2)}) async-start(s8[7340032]{0:T(1024)(128)(4,1)} %bitcast.44), calls=%async_computation.2 | async-start | bytes 8388608
  20.2 3.3 slice-start.3
  175.5 5.9 %copy-start.2 = (bf16[256,3584]{1,0:T(8,128)(2,1)S(1)}, bf16[256,3584]{1,0:T(8,128)(2,1)}, u32[]{:S(2)}) copy-start(bf16[256,3584]{1,0:T(8,128)(2,1)} %get-tuple-element.23) | copy-start | bytes 5505028
  175.5 12.2 %slice-start.4 = ((s8[7340032]{0:T(1024)(128)(4,1)}), s8[4194304]{0:T(1024)(128)(4,1)S(1)}, s32[]{:S(2)}) async-start(s8[7340032]{0:T(1024)(128)(4,1)} %bitcast.46), calls=%async_computation.4 | async-start | bytes 8388608
  181.4 6.3 %slice-start.5 = ((s8[7340032]{0:T(1024)(128)(4,1)}), s8[3145728]{0:T(1024)(128)(4,1)S(1)}, s32[]{:S(2)}) async-start(s8[7340032]{0:T(1024)(128)(4,1)} %bitcast.46), calls=%async_computation.5 | async-start | bytes 6291456
  187.7 14.6 %copy-start.9 = (bf16[64,1024]{1,0:T(8,128)(2,1)S(1)}, bf16[64,1024]{1,0:T(8,128)(2,1)}, u32[]{:S(2)}) copy-start(bf16[64,1024]{1,0:T(8,128)(2,1)} %param.9) | copy-start | bytes 393220
  187.7 27.2 %copy-start = (bf16[256,3584]{1,0:T(8,128)(2,1)S(1)}, bf16[256,3584]{1,0:T(8,128)(2,1)}, u32[]{:S(2)}) copy-start(bf16[256,3584]{1,0:T(8,128)(2,1)} %get-tuple-element.24) | copy-start | bytes 5505028
  214.9 3.2 copy-start.8
  224.9 5.4 %copy-start.7 = (bf16[256,1024]{1,0:T(8,128)(2,1)S(1)}, bf16[256,1024]{1,0:T(8,128)(2,1)}, u32[]{:S(2)}) copy-start(bf16[256,1024]{1,0:T(8,128)(2,1)} %get-tuple-element.27) | copy-start | bytes 1572868
  224.9 12.1 %slice-start.6 = ((s8[7340032]{0:T(1024)(128)(4,1)}), s8[4194304]{0:T(1024)(128)(4,1)S(1)}, s32[]{:S(2)}) async-start(s8[7340032]{0:T(1024)(128)(4,1)} %bitcast.48), calls=%async_computation.6 | async-start | bytes 8388608
  230.3 6.7 %slice-start.7 = ((s8[7340032]{0:T(1024)(128)(4,1)}), s8[3145728]{0:T(1024)(128)(4,1)S(1)}, s32[]{:S(2)}) async-start(s8[7340032]{0:T(1024)(128)(4,1)} %bitcast.48), calls=%async_computation.7 | async-start | bytes 6291456
  237.0 61.2 %copy-start.3 = (f32[32,3584]{1,0:T(8,128)S(1)}, f32[32,3584]{1,0:T(8,128)}, u32[]{:S(2)}) copy-start(f32[32,3584]{1,0:T(8,128)} %get-tuple-element.19) | copy-start | bytes 1376260
  237.0 61.2 %copy-start.4 = (f32[32,3584]{1,0:T(8,128)S(1)}, f32[32,3584]{1,0:T(8,128)}, u32[]{:S(2)}) copy-start(f32[32,3584]{1,0:T(8,128)} %get-tuple-element.20) | copy-start | bytes 1376260
  237.0 61.2 %copy-start.5 = (f32[32,3584]{1,0:T(8,128)S(1)}, f32[32,3584]{1,0:T(8,128)}, u32[]{:S(2)}) copy-start(f32[32,3584]{1,0:T(8,128)} %get-tuple-element.21) | copy-start | bytes 1376260
  237.0 61.2 %copy-start.6 = (f32[32,3584]{1,0:T(8,128)S(1)}, f32[32,3584]{1,0:T(8,128)}, u32[]{:S(2)}) copy-start(f32[32,3584]{1,0:T(8,128)} %get-tuple-element.22) | copy-start | bytes 1376260
where the time goes:
time: 364 us; the launch traced here: 361 us
  Pallas kernels  296 us (81%)
  matrix products  57.1 us (16%)
  other arithmetic  6.57 us (2%)
    pallas_call x3, Pallas kernels, scatter_sum(): pl.pallas_call(functools.partial(scatter_kernel, axis, count, arrays), ou...  165 us
    pallas_call x4, Pallas kernels, gather(): pl.pallas_call(functools.partial(gather_kernel, axis, count, arrays), out...  121 us
    dot_general x7, matrix products, matmul(): return jnp.dot(left, right, preferred_element_type=jnp.float32)  31.8 us
    dot_general x3, matrix products, tail_dot(): lax.dot_general(left, right, (((1,), (1,)), ((), ())), preferred_element_...  15.4 us
    dot_general x2, matrix products, lead_dot(): lax.dot_general(left, right, (((0,), (0,)), ((), ())), preferred_element_...  9.94 us
    pallas_call x1, Pallas kernels, weight_products(): pl.pallas_call(products_kernel, grid=(width // tile,), in_specs=[pl.Block...  9.41 us

commit v1 on v0

--- a/solution.py
+++ b/solution.py
@@ -226,21 +226,477 @@
     )(*parts)
 
 
+def ring_width(width):
+    return next(size for size in (256, 128) if width % size == 0)
+
+
+def between(value, low, high):
+    return jnp.logical_and(value >= low, value < high)
+
+
+def stream_kernel(axis, plan, *refs):
+    count, rows, width, chunk = plan.count, plan.rows, plan.width, plan.chunk
+    line, group, steps = count // 2, rows // 4, width // chunk
+    last = line - 1
+    ins, outs = refs[: plan.n_ins], refs[plan.n_ins : plan.n_ins + plan.n_outs]
+    rest = refs[plan.n_ins + plan.n_outs :]
+    (part, y_out, y_in, a_out, a_in, b_out, b_in, f_out, f_in) = rest[:9]
+    (y_s, y_r, a_s, a_r, b_s, b_r, f_s, f_r, h_s, h_r, g_s, g_r, x_s, x_r, k_s, k_r) = rest[9:25]
+    extra = rest[25:]
+    full0, full1 = outs[0], outs[1]
+    na, nb = plan.pair_first, plan.line_first
+
+    me = lax.axis_index(axis)
+    spot = lax.div(me, 2)
+    side = lax.rem(me, 2)
+    partner = me + 1 - 2 * side
+    at_end = jnp.logical_or(spot == 0, spot == last)
+    end = jnp.where(spot == 0, 0, 1)
+    place = [last - spot, spot]
+
+    barrier = pltpu.get_barrier_semaphore()
+
+    def greet(peer):
+        pl.semaphore_signal(
+            barrier, inc=1, device_id={axis: peer}, device_id_type=pl.DeviceIdType.MESH
+        )
+
+    greet(partner)
+    pl.when(spot > 0)(lambda: greet(me - 2))
+    pl.when(spot < last)(lambda: greet(me + 2))
+    work = plan.setup(ins, outs, extra)
+    pl.semaphore_wait(barrier, jnp.where(at_end, 2, 3))
+
+    def remote(src, dst, send, recv, peer):
+        return pltpu.make_async_remote_copy(
+            src_ref=src,
+            dst_ref=dst,
+            send_sem=send,
+            recv_sem=recv,
+            device_id={axis: peer},
+            device_id_type=pl.DeviceIdType.MESH,
+        )
+
+    def rows_of(e, s):
+        return pl.ds(pl.multiple_of((e * 2 + s) * group, group), group)
+
+    def cols_of(j):
+        return pl.ds(pl.multiple_of(j * chunk, chunk), chunk)
+
+    def y_copy(j):
+        return remote(y_out.at[j], y_in.at[j], y_s.at[j], y_r.at[j], partner)
+
+    def a_copy(d, j):
+        return remote(a_out.at[d, j], a_in.at[d, j], a_s.at[d, j], a_r.at[d, j], me - 2 + 4 * d)
+
+    def b_copy(d, j):
+        return remote(b_out.at[d, j], b_in.at[d, j], b_s.at[d, j], b_r.at[d, j], me - 2 + 4 * d)
+
+    def f_copy(j):
+        return remote(f_out.at[j], f_in.at[j], f_s.at[j], f_r.at[j], partner)
+
+    def h_copy(d, j):
+        block = full0.at[rows_of(1 - d, side), cols_of(j)]
+        return remote(block, block, h_s.at[d, j], h_r.at[d, j], me - 2 + 4 * d)
+
+    def g_copy(d, j):
+        block = full0.at[rows_of(1 - d, side), cols_of(j)]
+        return remote(block, block, g_s.at[d, j], g_r.at[d, j], partner)
+
+    def x_copy(j):
+        block = full1.at[rows_of(end, side), cols_of(j)]
+        return remote(block, block, x_s.at[j], x_r.at[j], partner)
+
+    def k_copy(d, j):
+        block = full1.at[pl.ds((1 - d) * 2 * group, 2 * group), cols_of(j)]
+        return remote(block, block, k_s.at[d, j], k_r.at[d, j], me - 2 + 4 * d)
+
+    def step(t, carry):
+        for d in (0, 1):
+            p = place[d]
+            jk = t - line - 1 - p
+            go = between(jk, 0, steps)
+
+            @pl.when(jnp.logical_and(go, p > 0))
+            def _():
+                k_copy(d, jk).wait_recv()
+
+            @pl.when(jnp.logical_and(go, p == 0))
+            def _():
+                x_copy(jk).wait_recv()
+
+            @pl.when(jnp.logical_and(go, p < last))
+            def _():
+                k_copy(d, jk).start()
+
+            jh = t - line - p
+
+            @pl.when(jnp.logical_and(between(jh, 0, steps), p > 0))
+            def _():
+                h_copy(d, jh).wait_recv()
+                g_copy(d, jh).start()
+
+            @pl.when(jnp.logical_and(between(jh, 0, steps), between(p, 1, last)))
+            def _():
+                h_copy(d, jh).start()
+
+            @pl.when(go)
+            def _():
+                g_copy(d, jk).wait_recv()
+
+        jc = t - line
+
+        @pl.when(jnp.logical_and(between(jc, 0, steps), at_end))
+        def _():
+            a_copy(end, jc).wait_recv()
+            f_copy(jc).wait_recv()
+            mine = rows_of(end, side)
+            sums = [None] * (len(na) + len(nb))
+            for i, a in enumerate(na):
+                sums[a] = part[a, jc, mine, :] + a_in[end, jc, i].astype(jnp.float32)
+            for i, a in enumerate(nb):
+                sums[a] = part[a, jc, mine, :] + f_in[jc, i].astype(jnp.float32)
+            first, second = plan.combine(ins, outs, cols_of(jc), sums)
+            full0[mine, cols_of(jc)] = first
+            full1[mine, cols_of(jc)] = second
+            x_copy(jc).start()
+
+        for d in (0, 1):
+
+            @pl.when(jnp.logical_and(between(jc, 0, steps), place[d] == 0))
+            def _():
+                h_copy(d, jc).start()
+                g_copy(d, jc).start()
+
+        for d in (0, 1):
+            p = place[d]
+            jb = t - p
+            slab = pl.ds(d * 2 * group, 2 * group)
+
+            @pl.when(jnp.logical_and(between(jb, 0, steps), between(p, 1, last)))
+            def _():
+                b_copy(d, jb).wait_recv()
+                for i, a in enumerate(nb):
+                    b_out[d, jb, i] = (
+                        part[a, jb, slab, :] + b_in[d, jb, i].astype(jnp.float32)
+                    ).astype(jnp.bfloat16)
+                b_copy(d, jb).start()
+
+            @pl.when(jnp.logical_and(between(jb, 0, steps), p == last))
+            def _():
+                b_copy(d, jb).wait_recv()
+                own = pl.ds(pl.multiple_of(side * group, group), group)
+                other = pl.ds(pl.multiple_of((1 - side) * group, group), group)
+                for i, a in enumerate(nb):
+                    f_out[jb, i] = (
+                        part[a, jb, rows_of(d, 1 - side), :]
+                        + b_in[d, jb, i, other, :].astype(jnp.float32)
+                    ).astype(jnp.bfloat16)
+                f_copy(jb).start()
+                for i, a in enumerate(nb):
+                    part[a, jb, rows_of(d, side), :] += b_in[d, jb, i, own, :].astype(jnp.float32)
+
+        jy = t - 1
+
+        @pl.when(between(jy, 0, steps))
+        def _():
+            y_copy(jy).wait_recv()
+            for i, a in enumerate(na):
+                for e in (0, 1):
+                    part[a, jy, rows_of(e, side), :] += y_in[jy, i, e].astype(jnp.float32)
+
+        for d in (0, 1):
+            p = place[d]
+            ja = t - 1 - p
+
+            @pl.when(jnp.logical_and(between(ja, 0, steps), between(p, 1, last)))
+            def _():
+                a_copy(d, ja).wait_recv()
+                for i, a in enumerate(na):
+                    a_out[d, ja, i] = (
+                        part[a, ja, rows_of(d, side), :] + a_in[d, ja, i].astype(jnp.float32)
+                    ).astype(jnp.bfloat16)
+                a_copy(d, ja).start()
+
+            @pl.when(jnp.logical_and(between(ja, 0, steps), p == 0))
+            def _():
+                for i, a in enumerate(na):
+                    a_out[d, ja, i] = part[a, ja, rows_of(d, side), :].astype(jnp.bfloat16)
+                a_copy(d, ja).start()
+
+        @pl.when(t < steps)
+        def _():
+            plan.produce(work, t, part)
+            for i, a in enumerate(na):
+                for e in (0, 1):
+                    y_out[t, i, e] = part[a, t, rows_of(e, 1 - side), :].astype(jnp.bfloat16)
+            y_copy(t).start()
+
+        for d in (0, 1):
+
+            @pl.when(jnp.logical_and(t < steps, place[d] == 0))
+            def _():
+                for i, a in enumerate(nb):
+                    b_out[d, t, i] = part[a, t, pl.ds(d * 2 * group, 2 * group), :].astype(
+                        jnp.bfloat16
+                    )
+                b_copy(d, t).start()
+
+        if plan.consume is not None:
+            jd = t - 2 * line
+
+            @pl.when(between(jd, 0, steps))
+            def _():
+                plan.consume(work, jd, full0, full1)
+
+        return carry
+
+    lax.fori_loop(0, steps + 2 * line, step, 0)
+
+    def settle(j, carry):
+        y_copy(j).wait_send()
+
+        @pl.when(at_end)
+        def _():
+            f_copy(j).wait_send()
+            x_copy(j).wait_send()
+
+        for d in (0, 1):
+            g_copy(d, j).wait_send()
+
+            @pl.when(place[d] < last)
+            def _():
+                a_copy(d, j).wait_send()
+                b_copy(d, j).wait_send()
+                h_copy(d, j).wait_send()
+                k_copy(d, j).wait_send()
+
+        return carry
+
+    lax.fori_loop(0, steps, settle, 0)
+    if plan.finish is not None:
+        plan.finish(work, outs)
+
+
+class Plan:
+    def __init__(self, **fields):
+        self.__dict__.update(fields)
+
+
+def stream(plan, axis, collective_id, operands, in_specs, more_outs, more_scratch, flops):
+    count, rows, width, chunk = plan.count, plan.rows, plan.width, plan.chunk
+    group, steps = rows // 4, width // chunk
+    na, nb = len(plan.pair_first), len(plan.line_first)
+    vmem = pl.BlockSpec(memory_space=pltpu.VMEM)
+    full = jax.ShapeDtypeStruct((rows, width), jnp.bfloat16)
+    outs = [full, full, *more_outs]
+    plan.n_ins, plan.n_outs = len(operands), len(outs)
+
+    def travel(*shape):
+        return [pltpu.VMEM(shape, jnp.bfloat16)] * 2
+
+    def marks(*shape):
+        return [pltpu.SemaphoreType.DMA(shape)] * 2
+
+    return pl.pallas_call(
+        functools.partial(stream_kernel, axis, plan),
+        out_shape=outs,
+        in_specs=in_specs,
+        out_specs=[vmem] * len(outs),
+        scratch_shapes=[
+            pltpu.VMEM((na + nb, steps, rows, chunk), jnp.float32),
+            *travel(steps, na, 2, group, chunk),
+            *travel(2, steps, na, group, chunk),
+            *travel(2, steps, nb, 2 * group, chunk),
+            *travel(steps, nb, group, chunk),
+            *marks(steps),
+            *marks(2, steps),
+            *marks(2, steps),
+            *marks(steps),
+            *marks(2, steps),
+            *marks(2, steps),
+            *marks(steps),
+            *marks(2, steps),
+            *more_scratch,
+        ],
+        compiler_params=pltpu.CompilerParams(
+            collective_id=collective_id, has_side_effects=True, vmem_limit_bytes=67043328
+        ),
+        cost_estimate=pl.CostEstimate(
+            flops=flops, bytes_accessed=40 * rows * width, transcendentals=0
+        ),
+    )(*operands)
+
+
+class Feed:
+    def __init__(self, sources, slots, sems, steps, view):
+        self.sources, self.slots, self.sems = sources, slots, sems
+        self.steps, self.view = steps, view
+        for j in range(min(2, steps)):
+            for copy in self.copies(j):
+                copy.start()
+
+    def copies(self, j):
+        slot = lax.rem(j, 3)
+        return [
+            pltpu.make_async_copy(
+                self.view(source, j), self.slots.at[slot, i], self.sems.at[slot, i]
+            )
+            for i, source in enumerate(self.sources)
+        ]
+
+    def take(self, j):
+        for copy in self.copies(j):
+            copy.wait()
+
+        @pl.when(j + 2 < self.steps)
+        def _():
+            for copy in self.copies(j + 2):
+                copy.start()
+
+        return self.slots.at[lax.rem(j, 3)]
+
+
+def forward(x, w_gate, w_up, t_gate, t_up, w_down, t_down):
+    count = lax.axis_size("gx")
+    rows, depth = x.shape
+    width = w_gate.shape[1]
+    model = w_down.shape[1]
+    chunk = ring_width(width)
+    steps, group = width // chunk, rows // 4
+
+    def setup(ins, outs, extra):
+        up_slots, up_sems, down_slots, down_sems, totals = extra
+        up = Feed(
+            ins[1:5],
+            up_slots,
+            up_sems,
+            steps,
+            lambda ref, j: ref.at[:, pl.ds(pl.multiple_of(j * chunk, chunk), chunk)],
+        )
+        down = Feed(
+            ins[5:7],
+            down_slots,
+            down_sems,
+            steps,
+            lambda ref, j: ref.at[pl.ds(pl.multiple_of(j * chunk, chunk), chunk), :],
+        )
+        totals[...] = jnp.zeros_like(totals)
+        return ins[0], up, down, totals
+
+    def produce(work, j, part):
+        x_ref, up, _, _ = work
+        weights = up.take(j)
+        for i in range(4):
+            part[i, j] = matmul(x_ref[...], weights[i])
+
+    def combine(ins, outs, columns, sums):
+        for i in range(4):
+            outs[2][i, :, columns] = sums[i]
+        gate, upper, gate_dot, upper_dot = sums
+        silu_val, first, _ = silu_parts(gate)
+        hidden = (silu_val * upper).astype(jnp.bfloat16)
+        hidden_dot = (first * gate_dot * upper + silu_val * upper_dot).astype(jnp.bfloat16)
+        return hidden, hidden_dot
+
+    def consume(work, j, full0, full1):
+        _, _, down, totals = work
+        weights = down.take(j)
+        columns = pl.ds(pl.multiple_of(j * chunk, chunk), chunk)
+        hidden, hidden_dot = full0[:, columns], full1[:, columns]
+        totals[0] += matmul(hidden, weights[0])
+        totals[1] += matmul(hidden_dot, weights[0]) + matmul(hidden, weights[1])
+
+    def finish(work, outs):
+        totals = work[3]
+        outs[3][...] = totals[0].astype(jnp.bfloat16)
+        outs[4][...] = totals[1].astype(jnp.bfloat16)
+
+    plan = Plan(
+        count=count, rows=rows, width=width, chunk=chunk,
+        pair_first=(0, 2), line_first=(1, 3),
+        setup=setup, produce=produce, combine=combine, consume=consume, finish=finish,
+    )
+    any_spec = pl.BlockSpec(memory_space=pl.ANY)
+    return stream(
+        plan, "gx", 1,
+        [x, w_gate, w_up, t_gate, t_up, w_down, t_down],
+        [pl.BlockSpec(memory_space=pltpu.VMEM)] + [any_spec] * 6,
+        [
+            jax.ShapeDtypeStruct((4, group, width), jnp.float32),
+            jax.ShapeDtypeStruct((rows, model), jnp.bfloat16),
+            jax.ShapeDtypeStruct((rows, model), jnp.bfloat16),
+        ],
+        [
+            pltpu.VMEM((3, 4, depth, chunk), jnp.bfloat16),
+            pltpu.SemaphoreType.DMA((3, 4)),
+            pltpu.VMEM((3, 2, chunk, model), jnp.bfloat16),
+            pltpu.SemaphoreType.DMA((3, 2)),
+            pltpu.VMEM((2, rows, model), jnp.float32),
+        ],
+        14 * rows * depth * width,
+    )
+
+
+def backward(grad, grad_dot, w_down, t_down, sums):
+    count = lax.axis_size("gx")
+    rows, model = grad.shape
+    width = w_down.shape[0]
+    chunk = ring_width(width)
+    steps = width // chunk
+
+    def setup(ins, outs, extra):
+        slots, sems = extra
+        feed = Feed(
+            ins[2:4],
+            slots,
+            sems,
+            steps,
+            lambda ref, j: ref.at[pl.ds(pl.multiple_of(j * chunk, chunk), chunk), :],
+        )
+        return ins[0], ins[1], feed
+
+    def produce(work, j, part):
+        grad_ref, grad_dot_ref, feed = work
+        weights = feed.take(j)
+        part[0, j] = tail_dot(grad_ref[...], weights[0])
+        part[1, j] = tail_dot(grad_dot_ref[...], weights[0]) + tail_dot(grad_ref[...], weights[1])
+
+    def combine(ins, outs, columns, arrived):
+        back, back_dot = arrived
+        gate, upper, gate_dot, upper_dot = [ins[4][i, :, columns] for i in range(4)]
+        silu_val, first, second = silu_parts(gate)
+        gate_in = (
+            back_dot * upper * first + back * upper_dot * first + back * upper * second * gate_dot
+        ).astype(jnp.bfloat16)
+        upper_in = (back_dot * silu_val + back * first * gate_dot).astype(jnp.bfloat16)
+        return gate_in, upper_in
+
+    plan = Plan(
+        count=count, rows=rows, width=width, chunk=chunk,
+        pair_first=(0,), line_first=(1,),
+        setup=setup, produce=produce, combine=combine, consume=None, finish=None,
+    )
+    vmem, any_spec = pl.BlockSpec(memory_space=pltpu.VMEM), pl.BlockSpec(memory_space=pl.ANY)
+    return stream(
+        plan, "gx", 3,
+        [grad, grad_dot, w_down, t_down, sums],
+        [vmem, vmem, any_spec, any_spec, vmem],
+        [],
+        [
+            pltpu.VMEM((3, 2, chunk, model), jnp.bfloat16),
+            pltpu.SemaphoreType.DMA((3, 2)),
+        ],
+        6 * rows * model * width,
+    )
+
+
 def body(tokens, target, w_gate, w_up, w_down, t_gate, t_up, t_down):
     scale = 1.0 / math.sqrt(TOKENS)
     (xfull,) = gather([tokens], "gy", 0)
-    rows = xfull
-    gate, upper, gate_dot, upper_dot = scatter_sum(
-        [matmul(rows, w) for w in (w_gate, w_up, t_gate, t_up)], "gx", 4
-    )
-    silu_val, first, second = silu_parts(gate)
-    hidden = (silu_val * upper).astype(jnp.bfloat16)
-    hidden_dot = (first * gate_dot * upper + silu_val * upper_dot).astype(jnp.bfloat16)
-    hid_full, hid_dot_full = gather([hidden, hidden_dot], "gx", 1)
-    rows = hid_full
-    rows_dot = hid_dot_full
-    output = matmul(rows, w_down)
-    output_dot = matmul(rows_dot, w_down) + matmul(rows, t_down)
+    hid_full, hid_dot_full, sums, output, output_dot = forward(
+        xfull, w_gate, w_up, t_gate, t_up, w_down, t_down
+    )
     output, output_dot = scatter_sum([output, output_dot], "gy", 6)
     grad = ((output - target.astype(jnp.float32)) * scale).astype(jnp.bfloat16)
     grad_dot = (output_dot * scale).astype(jnp.bfloat16)
@@ -248,16 +704,7 @@
     hvp_down = (lead_dot(hid_dot_full, grad_full) + lead_dot(hid_full, grad_dot_full)).astype(
         jnp.bfloat16
     )
-    rows = grad_full
-    rows_dot = grad_dot_full
-    back = tail_dot(rows, w_down)
-    back_dot = tail_dot(rows_dot, w_down) + tail_dot(rows, t_down)
-    back, back_dot = scatter_sum([back, back_dot], "gx", 5)
-    gate_in = (
-        back_dot * upper * first + back * upper_dot * first + back * upper * second * gate_dot
-    ).astype(jnp.bfloat16)
-    upper_in = (back_dot * silu_val + back * first * gate_dot).astype(jnp.bfloat16)
-    gate_full, upper_full = gather([gate_in, upper_in], "gx", 3)
+    gate_full, upper_full = backward(grad_full, grad_dot_full, w_down, t_down, sums)
     hvp_gate, hvp_up = weight_products(lax.optimization_barrier(xfull.T), gate_full, upper_full)
     return (hvp_gate, hvp_up, hvp_down)
 

time: 364 us -> 285 us (0.78)
  matrix products: 57.1 us -> 9 us
  Pallas kernels: 296 us -> 271 us
  other arithmetic: 6.57 us -> 1.81 us
    pallas_call x0 -> x2, Pallas kernels: none -> 229 us  [stream(): pl.pallas_call(functools.partial(stream_kernel, axis, plan), out_shape=ou...]
    pallas_call x3 -> x1, Pallas kernels: 165 us -> 11.5 us  [scatter_sum(): pl.pallas_call(functools.partial(scatter_kernel, axis, count, arrays), ou...]
    pallas_call x4 -> x2, Pallas kernels: 121 us -> 20.4 us  [gather(): pl.pallas_call(functools.partial(gather_kernel, axis, count, arrays), out...]
    dot_general x10 -> x0, matrix products: 47.1 us -> none  [the longest x7 31.8 us: matmul(): return jnp.dot(left, right, preferred_element_type=jnp.float32)]
    convert_element_type x2 -> x0, other arithmetic: 4.78 us -> none  [the longest x1 2.44 us: body(): (first * gate_dot * upper + silu_val * upper_dot).astype(jnp.bfloat16)]
where the time goes in v1:
time: 285 us; the launch traced here: 284 us
  Pallas kernels  271 us (95%)
  matrix products  9 us (3%)
    pallas_call x2, Pallas kernels, stream(): pl.pallas_call(functools.partial(stream_kernel, axis, plan), out_shape=ou...  229 us
    pallas_call x2, Pallas kernels, gather(): pl.pallas_call(functools.partial(gather_kernel, axis, count, arrays), out...  20.4 us
    pallas_call x1, Pallas kernels, scatter_sum(): pl.pallas_call(functools.partial(scatter_kernel, axis, count, arrays), ou...  11.5 us
    pallas_call x1, Pallas kernels, weight_products(): pl.pallas_call(products_kernel, grid=(width // tile,), in_specs=[pl.Block...  9.41 us
    dot_general x2, matrix products, lead_dot(): lax.dot_general(left, right, (((0,), (0,)), ((), ())), preferred_element_...  9 us

profile of v1, /device:TPU:0, one launch (start us, length us, event | category | flops | bytes accessed | tf_op | source)
XLA Modules:
  0.0 284.2 jit_solution(9910238819268052703)
XLA Ops:
  0.6 9.5 %shard_map.103.refs_0_ = bf16[256,1024]{1,0:T(8,128)(2,1)} custom-call(bf16[64,1024]{1,0:T(8,128)(2,1)} %refs_0_.1), custom_call_target="tpu_custom_call" | custom-call | bytes 6291456 | tf_op jit(solution)/shard_map/pallas_call | solution.py:99
  10.2 130.1 %shard_map.104 = (bf16[256,3584]{1,0:T(8,128)(2,1)}, bf16[256,3584]{1,0:T(8,128)(2,1)}, f32[4,64,3584]{2,1,0:T(8,128)}, bf16[256,1024]{1,0:T(8,128)(2,1)}, bf16[256,1024]{1,0:T(8,128)(2,1)}) custom-call(bf16[256,1024]{1,0:T(8,128)(2,1)} %shard_map.103.refs_0_, bf16[1024,3584]{1,0:T(8,128)(2,1)} %refs_1_.1, bf16[1024,3584]{1,0:T(8,128)(2,1)} %refs_2_.2, ...), custom_call_target="tpu_custom_call" | custom-call | flops 13153337344 | bytes 36700160 | tf_op jit(solution)/shard_map/pallas_call | solution.py:501
  140.3 11.5 %shard_map.105 = (f32[64,1024]{1,0:T(8,128)}, f32[64,1024]{1,0:T(8,128)}) custom-call(bf16[4,64,1024]{2,1,0:T(8,128)(2,1)} %bitcast.7, bf16[4,64,1024]{2,1,0:T(8,128)(2,1)} %bitcast.8), custom_call_target="tpu_custom_call" | custom-call | bytes 12582912 | tf_op jit(solution)/shard_map/pallas_call | solution.py:211
  151.8 1.8 multiply_convert_fusion
  153.6 10.9 %shard_map.106 = (bf16[256,1024]{1,0:T(8,128)(2,1)}, bf16[256,1024]{1,0:T(8,128)(2,1)}) custom-call(bf16[64,1024]{1,0:T(8,128)(2,1)} %get-tuple-element.30.refs_0_, bf16[64,1024]{1,0:T(8,128)(2,1)} %get-tuple-element.29.refs_1_), custom_call_target="tpu_custom_call" | custom-call | bytes 12582912 | tf_op jit(solution)/shard_map/pallas_call | solution.py:99
  164.5 0.0 copy-start
  164.5 0.0 copy-start.1
  164.5 3.8 %fusion = f32[3584,1024]{1,0:T(8,128)S(1)} fusion(bf16[256,3584]{1,0:T(8,128)(2,1)} %get-tuple-element.27, bf16[256,1024]{1,0:T(8,128)(2,1)} %get-tuple-element.20.refs_0_), kind=kOutput, calls=%fused_computation.3 | convolution fusion | flops 1879048192 | bytes 17039360 | tf_op jit(solution)/shard_map/dot_general | solution.py:26
  168.3 0.0 copy-done
  168.3 0.0 copy-done.1
  168.3 5.2 %add_convert_fusion = bf16[3584,1024]{1,0:T(8,128)(2,1)} fusion(f32[3584,1024]{1,0:T(8,128)S(1)} %fusion, bf16[256,3584]{1,0:T(8,128)(2,1)S(1)} %copy-done, bf16[256,1024]{1,0:T(8,128)(2,1)S(1)} %copy-done.1), kind=kOutput, calls=%fused_computation | convolution fusion | flops 1886388224 | bytes 24379392 | tf_op jit(solution)/shard_map/dot_general | solution.py:26
  173.5 99.2 %shard_map.107 = (bf16[256,3584]{1,0:T(8,128)(2,1)}, bf16[256,3584]{1,0:T(8,128)(2,1)}) custom-call(bf16[256,1024]{1,0:T(8,128)(2,1)} %get-tuple-element.20.refs_0_, bf16[256,1024]{1,0:T(8,128)(2,1)} %get-tuple-element.21.refs_1_, bf16[3584,1024]{1,0:T(8,128)(2,1)} %refs_2_.3, bf16[3584,1024]{1,0:T(8,128)(2,1)} %refs_3_.3, ...), custom_call_target="tpu_custom_call" | custom-call | flops 5637144576 | bytes 36700160 | tf_op jit(solution)/shard_map/pallas_call | solution.py:501
  272.7 2.0 copy.11
  274.8 9.4 %shard_map.108 = (bf16[1024,3584]{1,0:T(8,128)(2,1)}, bf16[1024,3584]{1,0:T(8,128)(2,1)}) custom-call(bf16[1024,256]{1,0:T(8,128)(2,1)} %bitcast.9, bf16[256,3584]{1,0:T(8,128)(2,1)} %get-tuple-element.23.gate, bf16[256,3584]{1,0:T(8,128)(2,1)} %get-tuple-element.24.upper), custom_call_target="tpu_custom_call" | custom-call | flops 3758096384 | bytes 18350080 | tf_op jit(solution)/shard_map/pallas_call | solution.py:130
Async XLA Ops:
  164.5 3.9 %copy-start = (bf16[256,3584]{1,0:T(8,128)(2,1)S(1)}, bf16[256,3584]{1,0:T(8,128)(2,1)}, u32[]{:S(2)}) copy-start(bf16[256,3584]{1,0:T(8,128)(2,1)} %get-tuple-element.28) | copy-start | bytes 5505028
  164.5 3.9 %copy-start.1 = (bf16[256,1024]{1,0:T(8,128)(2,1)S(1)}, bf16[256,1024]{1,0:T(8,128)(2,1)}, u32[]{:S(2)}) copy-start(bf16[256,1024]{1,0:T(8,128)(2,1)} %get-tuple-element.21.refs_1_) | copy-start | bytes 1572868

commit v2 on v0

v2 whole, which is shorter than its diff:
```python
import functools
import math

import jax
import jax.numpy as jnp
from jax import lax
from jax.experimental import pallas as pl
from jax.experimental.pallas import tpu as pltpu
from jax.sharding import PartitionSpec as P

TOKENS = 256
CHUNKS = (512, 256, 128)
F32, BF16 = jnp.float32, jnp.bfloat16


def silu_parts(gate):
    sig = jax.nn.sigmoid(gate)
    first = sig * (1.0 + gate * (1.0 - sig))
    second = sig * (1.0 - sig) * (2.0 + gate * (1.0 - 2.0 * sig))
    return (gate * sig, first, second)


def matmul(left, right):
    return jnp.dot(left, right, preferred_element_type=F32)


def lead_dot(left, right):
    return lax.dot_general(left, right, (((0,), (0,)), ((), ())), preferred_element_type=F32)


def tail_dot(left, right):
    return lax.dot_general(left, right, (((1,), (1,)), ((), ())), preferred_element_type=F32)


def between(value, low, high):
    return jnp.logical_and(value >= low, value < high)


def both(*terms):
    return functools.reduce(jnp.logical_and, terms)


def span(start, size):
    return pl.ds(pl.multiple_of(start * size, size), size)


def remote(src, dst, sems, index, axis, peer):
    return pltpu.make_async_remote_copy(
        src_ref=src,
        dst_ref=dst,
        send_sem=sems[0].at[index],
        recv_sem=sems[1].at[index],
        device_id={axis: peer},
        device_id_type=pl.DeviceIdType.MESH,
    )


class Sizes:
    def __init__(self, tokens, w_gate):
        self.line = lax.axis_size("gx") // 2
        self.gy = lax.axis_size("gy")
        self.pairs = self.gy // 2
        own, self.depth = tokens.shape
        self.width = w_gate.shape[1]
        self.halves = 2 if own % 32 == 0 else 1
        self.own = own // self.halves
        self.rows = self.own * self.gy
        self.group = self.rows // 4
        self.chunk = next(size for size in CHUNKS if self.width % size == 0)
        self.steps = self.width // self.chunk
        self.items = self.halves * self.steps


class Stream:
    def __init__(self, sizes, na, nb):
        self.z, self.na, self.nb = sizes, na, nb

    def scratch(self):
        z, na, nb = self.z, self.na, self.nb
        n, g, c = z.items, z.group, z.chunk
        sem = pltpu.SemaphoreType.DMA
        pairs = [(n,), (2, n), (2, n), (n,), (2, n), (2, n), (n,), (2, n)]
        return [
            pltpu.VMEM((na + nb, z.line, z.rows, c), F32),
            pltpu.VMEM((n, na, 2, g, c), BF16),
            pltpu.VMEM((n, na, 2, g, c), BF16),
            pltpu.VMEM((2, n, na, g, c), BF16),
            pltpu.VMEM((2, n, nb, 2 * g, c), BF16),
            pltpu.VMEM((n, nb, g, c), BF16),
            pltpu.VMEM((n, nb, g, c), BF16),
            *[sem(shape) for shape in pairs for _ in range(2)],
        ]

    def bind(self, refs, full0, full1, produce, combine, consume):
        self.part, self.y_out, self.y_in, self.a, self.b, self.f_out, self.f_in = refs[:7]
        sems = [(refs[7 + 2 * i], refs[8 + 2 * i]) for i in range(8)]
        (self.ys, self.as_, self.bs, self.fs, self.hs, self.gs, self.xs, self.ks) = sems
        self.full0, self.full1 = full0, full1
        self.produce, self.combine, self.consume = produce, combine, consume
        z = self.z
        self.me = lax.axis_index("gx")
        self.spot, self.side = lax.div(self.me, 2), lax.rem(self.me, 2)
        self.partner = self.me + 1 - 2 * self.side
        self.last = z.line - 1
        self.at_end = jnp.logical_or(self.spot == 0, self.spot == self.last)
        self.end = jnp.where(self.spot == 0, 0, 1)
        self.place = [self.last - self.spot, self.spot]

    def group_of(self, e, s):
        return span(e * 2 + s, self.z.group)

    def block(self, full, k, e, s):
        z = self.z
        half, j = lax.div(k, z.steps), lax.rem(k, z.steps)
        return full.at[span(half * 4 + e * 2 + s, z.group), span(j, z.chunk)]

    def slab(self, full, k, e):
        z = self.z
        half, j = lax.div(k, z.steps), lax.rem(k, z.steps)
        return full.at[span(half * 2 + e, 2 * z.group), span(j, z.chunk)]

    def across(self, src, dst, sems, index):
        return remote(src, dst, sems, index, "gx", self.partner)

    def along(self, d, src, dst, sems, index):
        return remote(src, dst, sems, index, "gx", self.me - 2 + 4 * d)

    def y_copy(self, k):
        return self.across(self.y_out.at[k], self.y_in.at[k], self.ys, k)

    def f_copy(self, k):
        return self.across(self.f_out.at[k], self.f_in.at[k], self.fs, k)

    def a_copy(self, d, k):
        return self.along(d, self.a.at[d, k], self.a.at[d, k], self.as_, (d, k))

    def b_copy(self, d, k):
        return self.along(d, self.b.at[d, k], self.b.at[d, k], self.bs, (d, k))

    def h_copy(self, d, k):
        block = self.block(self.full0, k, 1 - d, self.side)
        return self.along(d, block, block, self.hs, (d, k))

    def g_copy(self, d, k):
        block = self.block(self.full0, k, 1 - d, self.side)
        return self.across(block, block, self.gs, (d, k))

    def x_copy(self, k):
        block = self.block(self.full1, k, self.end, self.side)
        return self.across(block, block, self.xs, k)

    def k_copy(self, d, k):
        block = self.slab(self.full1, k, 1 - d)
        return self.along(d, block, block, self.ks, (d, k))

    def early(self, t):
        z, last, side, na, nb = self.z, self.last, self.side, self.na, self.nb
        n, part, a, b = z.items, self.part, self.a, self.b
        for d in (0, 1):
            p = self.place[d]
            k, h = t - z.line - 1 - p, t - z.line - p
            go = between(k, 0, n)

            @pl.when(both(go, p > 0))
            def _():
                self.k_copy(d, k).wait_recv()

            @pl.when(both(go, p == 0))
            def _():
                self.x_copy(k).wait_recv()

            @pl.when(both(go, p < last))
            def _():
                self.k_copy(d, k).start()

            @pl.when(both(between(h, 0, n), p > 0))
            def _():
                self.h_copy(d, h).wait_recv()
                self.g_copy(d, h).start()

            @pl.when(both(between(h, 0, n), between(p, 1, last)))
            def _():
                self.h_copy(d, h).start()

            @pl.when(go)
            def _():
                self.g_copy(d, k).wait_recv()

        k = t - z.line

        @pl.when(both(between(k, 0, n), self.at_end))
        def _():
            self.a_copy(self.end, k).wait_recv()
            self.f_copy(k).wait_recv()
            slot, mine = lax.rem(k, z.line), self.group_of(self.end, side)
            sums = [part[i, slot, mine, :] + a[self.end, k, i].astype(F32) for i in range(na)]
            sums += [part[na + i, slot, mine, :] + self.f_in[k, i].astype(F32) for i in range(nb)]
            first, second = self.combine(k, sums)
            self.block(self.full0, k, self.end, side)[...] = first
            self.block(self.full1, k, self.end, side)[...] = second
            self.x_copy(k).start()
            self.h_copy(1 - self.end, k).start()
            self.g_copy(1 - self.end, k).start()

        for d in (0, 1):
            p = self.place[d]
            k = t - p

            @pl.when(both(between(k, 0, n), between(p, 1, last)))
            def _():
                self.b_copy(d, k).wait_recv()
                slot, slab = lax.rem(k, z.line), span(d, 2 * z.group)
                for i in range(nb):
                    b[d, k, i] = (part[na + i, slot, slab, :] + b[d, k, i].astype(F32)).astype(BF16)
                self.b_copy(d, k).start()

            @pl.when(both(between(k, 0, n), p == last))
            def _():
                self.b_copy(d, k).wait_recv()
                slot = lax.rem(k, z.line)
                own, other = span(side, z.group), span(1 - side, z.group)
                for i in range(nb):
                    self.f_out[k, i] = (
                        part[na + i, slot, self.group_of(d, 1 - side), :]
                        + b[d, k, i, other, :].astype(F32)
                    ).astype(BF16)
                self.f_copy(k).start()
                for i in range(nb):
                    part[na + i, slot, self.group_of(d, side), :] += b[d, k, i, own, :].astype(F32)

        k = t - 1

        @pl.when(between(k, 0, n))
        def _():
            self.y_copy(k).wait_recv()
            for i in range(na):
                for e in (0, 1):
                    part[i, lax.rem(k, z.line), self.group_of(e, side), :] += self.y_in[
                        k, i, e
                    ].astype(F32)

        for d in (0, 1):
            p = self.place[d]
            k = t - 1 - p

            @pl.when(both(between(k, 0, n), between(p, 1, last)))
            def _():
                self.a_copy(d, k).wait_recv()
                for i in range(na):
                    a[d, k, i] = (
                        part[i, lax.rem(k, z.line), self.group_of(d, side), :]
                        + a[d, k, i].astype(F32)
                    ).astype(BF16)
                self.a_copy(d, k).start()

            @pl.when(both(between(k, 0, n), p == 0))
            def _():
                for i in range(na):
                    a[d, k, i] = part[i, lax.rem(k, z.line), self.group_of(d, side), :].astype(BF16)
                self.a_copy(d, k).start()

    def late(self, t):
        z, na, nb = self.z, self.na, self.nb

        @pl.when(between(t, 0, z.items))
        def _():
            slot = lax.rem(t, z.line)
            self.produce(t, self.part, slot)
            for i in range(na):
                for e in (0, 1):
                    self.y_out[t, i, e] = self.part[
                        i, slot, self.group_of(e, 1 - self.side), :
                    ].astype(BF16)
            self.y_copy(t).start()

            @pl.when(self.at_end)
            def _():
                d = 1 - self.end
                for i in range(nb):
                    self.b[d, t, i] = self.part[na + i, slot, span(d, 2 * z.group), :].astype(BF16)
                self.b_copy(d, t).start()

        if self.consume is not None:
            k = t - 2 * z.line

            @pl.when(between(k, 0, z.items))
            def _():
                self.consume(k)

    def settle(self, k):
        self.y_copy(k).wait_send()

        @pl.when(self.at_end)
        def _():
            self.f_copy(k).wait_send()
            self.x_copy(k).wait_send()

        for d in (0, 1):
            self.g_copy(d, k).wait_send()

            @pl.when(self.place[d] < self.last)
            def _():
                self.a_copy(d, k).wait_send()
                self.b_copy(d, k).wait_send()
                self.h_copy(d, k).wait_send()
                self.k_copy(d, k).wait_send()


class Feed:
    def __init__(self, sources, slots, sems, sizes, view):
        self.sources, self.slots, self.sems = sources, slots, sems
        self.sizes, self.view = sizes, view

    def copies(self, k):
        slot, j = lax.rem(k, 2), lax.rem(k, self.sizes.steps)
        return [
            pltpu.make_async_copy(
                self.view(source, j), self.slots.at[slot, i], self.sems.at[slot, i]
            )
            for i, source in enumerate(self.sources)
        ]

    def start(self, k):
        for copy in self.copies(k):
            copy.start()

    def take(self, k):
        for copy in self.copies(k):
            copy.wait()
        pl.when(k + 1 < self.sizes.items)(lambda: self.start(k + 1))
        return self.slots.at[lax.rem(k, 2)]


def hvp_kernel(z, scale, forward, backward, *refs):
    tokens, target, w_gate, w_up, t_gate, t_up, w_down, t_down = refs[:8]
    x_full, hid, hid_dot, grads, gate_in, upper_in = refs[8:14]
    count = len(forward.scratch())
    f_refs, b_refs, rest = refs[14 : 14 + count], refs[14 + count : 14 + 2 * count], refs[14 + 2 * count :]
    up_slots, up_sems, down_slots, down_sems, back_slots, back_sems = rest[:6]
    totals, saved, m1_out, m1_in, m2_out, m2_in = rest[6:12]
    sems = [(rest[12 + 2 * i], rest[13 + 2 * i]) for i in range(8)]
    x1, x2, x3, m1, m2, m3, m3p, m4 = sems

    me = lax.axis_index("gy")
    core, pair = lax.rem(me, 2), lax.div(me, 2)
    other = me + 1 - 2 * core
    peers = [lax.rem(pair + s, z.pairs) * 2 + core for s in range(1, z.pairs)]
    sources = [lax.rem(pair + z.pairs - s, z.pairs) * 2 + core for s in range(1, z.pairs)]
    hops = range(z.pairs - 1)

    up = Feed((w_gate, w_up, t_gate, t_up), up_slots, up_sems, z, lambda r, j: r.at[:, span(j, z.chunk)])
    down = Feed((w_down, t_down), down_slots, down_sems, z, lambda r, j: r.at[span(j, z.chunk), :])
    again = Feed((w_down, t_down), back_slots, back_sems, z, lambda r, j: r.at[span(j, z.chunk), :])

    def half_rows(k):
        return span(lax.div(k, z.steps), z.rows)

    def produce_up(k, part, slot):
        weights = up.take(k)
        x = x_full[half_rows(k), :]
        for i in range(4):
            part[i, slot] = matmul(x, weights[(0, 2, 1, 3)[i]])

    def combine_up(k, sums):
        gate, gate_dot, upper, upper_dot = sums
        for i in range(4):
            saved[i, k] = sums[i]
        silu_val, first, _ = silu_parts(gate)
        return (
            (silu_val * upper).astype(BF16),
            (first * gate_dot * upper + silu_val * upper_dot).astype(BF16),
        )

    def consume_up(k):
        weights = down.take(k)
        half, columns = lax.div(k, z.steps), span(lax.rem(k, z.steps), z.chunk)
        hidden, hidden_dot = hid[half_rows(k), columns], hid_dot[half_rows(k), columns]
        totals[half, 0] += matmul(hidden, weights[0])
        totals[half, 1] += matmul(hidden_dot, weights[0]) + matmul(hidden, weights[1])

    def produce_back(k, part, slot):
        weights = again.take(k)
        grad, grad_dot = grads[0, half_rows(k), :], grads[1, half_rows(k), :]
        part[0, slot] = tail_dot(grad, weights[0])
        part[1, slot] = tail_dot(grad_dot, weights[0]) + tail_dot(grad, weights[1])

    def combine_back(k, sums):
        back, back_dot = sums
        gate, gate_dot, upper, upper_dot = [saved[i, k] for i in range(4)]
        silu_val, first, second = silu_parts(gate)
        return (
            (
                back_dot * upper * first + back * upper_dot * first + back * upper * second * gate_dot
            ).astype(BF16),
            (back_dot * silu_val + back * first * gate_dot).astype(BF16),
        )

    forward.bind(f_refs, hid, hid_dot, produce_up, combine_up, consume_up)
    backward.bind(b_refs, gate_in, upper_in, produce_back, combine_back, None)

    barrier = pltpu.get_barrier_semaphore()

    def greet(axis, peer):
        pl.semaphore_signal(
            barrier, inc=1, device_id={axis: peer}, device_id_type=pl.DeviceIdType.MESH
        )

    greet("gx", forward.partner)
    pl.when(forward.spot > 0)(lambda: greet("gx", forward.me - 2))
    pl.when(forward.spot < forward.last)(lambda: greet("gx", forward.me + 2))
    for peer in [other, *peers]:
        greet("gy", peer)
    up.start(0)
    down.start(0)
    again.start(0)
    totals[...] = jnp.zeros_like(totals)
    pl.semaphore_wait(barrier, z.pairs + jnp.where(forward.at_end, 2, 3))

    def x_rows(h, index):
        return x_full.at[span(h * z.gy + index, z.own)]

    def x_copy(h, s):
        return remote(tokens.at[span(h, z.own)], x_rows(h, me), x1, (h, s), "gy", peers[s])

    def x_side(h):
        return remote(tokens.at[span(h, z.own)], x_rows(h, me), x2, h, "gy", other)

    def x_pass(h, s):
        block = x_rows(h, sources[s])
        return remote(block, block, x3, (h, s), "gy", other)

    for h in range(z.halves):
        for s in hops:
            x_copy(h, s).start()
        x_side(h).start()
        x_rows(h, me)[...] = tokens[h * z.own : (h + 1) * z.own, :]
    for h in range(z.halves):
        for s in hops:
            x_copy(h, s).wait_recv()
            x_pass(h, s).start()
    for h in range(z.halves):
        x_side(h).wait_recv()
        for s in hops:
            x_pass(h, s).wait_recv()

    def own_rows(index):
        return span(index, z.own)

    def m1_copy(h):
        return remote(m1_out.at[h], m1_in.at[h], m1, h, "gy", other)

    def m2_copy(h, s):
        return remote(m2_out.at[h, s], m2_in.at[h, s], m2, (h, s), "gy", peers[s])

    def grad_rows(h, index):
        return grads.at[:, span(h * z.gy + index, z.own), :]

    def m3_copy(h, s):
        return remote(grad_rows(h, me), grad_rows(h, me), m3, (h, s), "gy", peers[s])

    def m3_side(h):
        return remote(grad_rows(h, me), grad_rows(h, me), m3p, h, "gy", other)

    def m4_copy(h, s):
        block = grad_rows(h, sources[s])
        return remote(block, block, m4, (h, s), "gy", other)

    ready = z.steps - 1 + 2 * z.line
    start_back = ready + 4

    def middle_send(t):
        for h in range(z.halves):

            @pl.when(t == ready + h * z.steps)
            def _():
                for i in (0, 1):
                    for g in range(z.pairs):
                        m1_out[h, i, g] = totals[h, i, own_rows(g * 2 + 1 - core), :].astype(BF16)
                m1_copy(h).start()

    def middle(t):
        for h in range(z.halves):
            base = ready + h * z.steps

            @pl.when(t == base + 1)
            def _():
                m1_copy(h).wait_recv()
                for i in (0, 1):
                    totals[h, i, own_rows(me), :] += m1_in[h, i, pair].astype(F32)
                for s in hops:
                    g = lax.div(peers[s], 2)
                    for i in (0, 1):
                        m2_out[h, s, i] = (
                            totals[h, i, own_rows(peers[s]), :] + m1_in[h, i, g].astype(F32)
                        ).astype(BF16)
                    m2_copy(h, s).start()

            @pl.when(t == base + 2)
            def _():
                outs = [totals[h, i, own_rows(me), :] for i in (0, 1)]
                for s in hops:
                    m2_copy(h, s).wait_recv()
                    outs = [outs[i] + m2_in[h, s, i].astype(F32) for i in (0, 1)]
                goal = target[h * z.own : (h + 1) * z.own, :].astype(F32)
                grad_rows(h, me)[0] = ((outs[0] - goal) * scale).astype(BF16)
                grad_rows(h, me)[1] = (outs[1] * scale).astype(BF16)
                for s in hops:
                    m3_copy(h, s).start()
                m3_side(h).start()

            @pl.when(t == base + 3)
            def _():
                for s in hops:
                    m3_copy(h, s).wait_recv()
                    m4_copy(h, s).start()

            @pl.when(t == base + 4)
            def _():
                m3_side(h).wait_recv()
                for s in hops:
                    m4_copy(h, s).wait_recv()

    def step(t, carry):
        forward.early(t)
        middle(t)
        backward.early(t - start_back)
        forward.late(t)
        middle_send(t)
        backward.late(t - start_back)
        return carry

    lax.fori_loop(0, start_back + z.items + 2 * z.line, step, 0)

    for h in range(z.halves):
        for s in hops:
            x_copy(h, s).wait_send()
            x_pass(h, s).wait_send()
            m2_copy(h, s).wait_send()
            m3_copy(h, s).wait_send()
            m4_copy(h, s).wait_send()
        x_side(h).wait_send()
        m1_copy(h).wait_send()
        m3_side(h).wait_send()

    def settle(k, carry):
        forward.settle(k)
        backward.settle(k)
        return carry

    lax.fori_loop(0, z.items, settle, 0)


def run(tokens, target, w_gate, w_up, w_down, t_gate, t_up, t_down):
    z = Sizes(tokens, w_gate)
    model = w_down.shape[1]
    tall = z.halves * z.rows
    forward, backward = Stream(z, 2, 2), Stream(z, 1, 1)
    vmem, any_spec = pl.BlockSpec(memory_space=pltpu.VMEM), pl.BlockSpec(memory_space=pl.ANY)
    sem = pltpu.SemaphoreType.DMA
    hops = max(z.pairs - 1, 1)
    wide = jax.ShapeDtypeStruct((tall, z.width), BF16)
    marks = [(z.halves, hops), (z.halves,), (z.halves, hops), (z.halves,), (z.halves, hops),
             (z.halves, hops), (z.halves,), (z.halves, hops)]
    return pl.pallas_call(
        functools.partial(hvp_kernel, z, 1.0 / math.sqrt(TOKENS), forward, backward),
        out_shape=[
            jax.ShapeDtypeStruct((tall, z.depth), BF16),
            wide,
            wide,
            jax.ShapeDtypeStruct((2, tall, model), BF16),
            wide,
            wide,
        ],
        in_specs=[vmem] * 2 + [any_spec] * 6,
        out_specs=[vmem] * 6,
        scratch_shapes=[
            *forward.scratch(),
            *backward.scratch(),
            pltpu.VMEM((2, 4, z.depth, z.chunk), BF16),
            sem((2, 4)),
            pltpu.VMEM((2, 2, z.chunk, model), BF16),
            sem((2, 2)),
            pltpu.VMEM((2, 2, z.chunk, model), BF16),
            sem((2, 2)),
            pltpu.VMEM((z.halves, 2, z.rows, model), F32),
            pltpu.VMEM((4, z.items, z.group, z.chunk), F32),
            pltpu.VMEM((z.halves, 2, z.pairs, z.own, model), BF16),
            pltpu.VMEM((z.halves, 2, z.pairs, z.own, model), BF16),
            pltpu.VMEM((z.halves, hops, 2, z.own, model), BF16),
            pltpu.VMEM((z.halves, hops, 2, z.own, model), BF16),
            *[sem(shape) for shape in marks for _ in range(2)],
        ],
        compiler_params=pltpu.CompilerParams(
            collective_id=0, has_side_effects=True, vmem_limit_bytes=67043328
        ),
        cost_estimate=pl.CostEstimate(
            flops=20 * tall * z.depth * z.width,
            bytes_accessed=60 * tall * z.width,
            transcendentals=0,
        ),
    )(tokens, target, w_gate, w_up, t_gate, t_up, w_down, t_down)


def products_kernel(turned, gate, upper, hidden, hidden_dot, grads, out_gate, out_up, out_down):
    out_gate[...] = matmul(turned[...], gate[...]).astype(BF16)
    out_up[...] = matmul(turned[...], upper[...]).astype(BF16)
    out_down[...] = (
        lead_dot(hidden_dot[...], grads[0]) + lead_dot(hidden[...], grads[1])
    ).astype(BF16)


def weight_products(turned, gate, upper, hidden, hidden_dot, grads):
    depth, rows = turned.shape
    width, model = gate.shape[1], grads.shape[2]
    tile = next(size for size in CHUNKS if width % size == 0)
    strip = pl.BlockSpec((rows, tile), lambda i: (0, i))
    return pl.pallas_call(
        products_kernel,
        grid=(width // tile,),
        in_specs=[
            pl.BlockSpec((depth, rows), lambda i: (0, 0)),
            *[strip] * 4,
            pl.BlockSpec((2, rows, model), lambda i: (0, 0, 0)),
        ],
        out_specs=[
            pl.BlockSpec((depth, tile), lambda i: (0, i)),
            pl.BlockSpec((depth, tile), lambda i: (0, i)),
            pl.BlockSpec((tile, model), lambda i: (i, 0)),
        ],
        out_shape=[
            jax.ShapeDtypeStruct((depth, width), BF16),
            jax.ShapeDtypeStruct((depth, width), BF16),
            jax.ShapeDtypeStruct((width, model), BF16),
        ],
        cost_estimate=pl.CostEstimate(
            flops=4 * rows * (depth + model) * width,
            bytes_accessed=2 * (2 * depth + model + 4 * rows) * width,
            transcendentals=0,
        ),
    )(turned, gate, upper, hidden, hidden_dot, grads)


def body(tokens, target, w_gate, w_up, w_down, t_gate, t_up, t_down):
    x_full, hidden, hidden_dot, grads, gate_in, upper_in = run(
        tokens, target, w_gate, w_up, w_down, t_gate, t_up, t_down
    )
    turned = lax.optimization_barrier(x_full.T)
    return tuple(weight_products(turned, gate_in, upper_in, hidden, hidden_dot, grads))


def solution(mesh):
    return jax.shard_map(
        body,
        mesh=mesh,
        in_specs=(
            P("gy", "gx"),
            P("gy", "gx"),
            P("gx", "gy"),
            P("gx", "gy"),
            P("gy", "gx"),
            P("gx", "gy"),
            P("gx", "gy"),
            P("gy", "gx"),
        ),
        out_specs=(P("gx", "gy"), P("gx", "gy"), P("gy", "gx")),
        check_vma=False,
    )
```

time: 364 us -> 242 us (0.66)
  matrix products: 57.1 us -> 0 us
  Pallas kernels: 296 us -> 239 us
  other arithmetic: 6.57 us -> 0 us
    pallas_call x7 -> x1, Pallas kernels: 286 us -> 225 us  [run(): pl.pallas_call(functools.partial(hvp_kernel, z, 1.0 / math.sqrt(TOKENS),...]
    dot_general x12 -> x0, matrix products: 57.1 us -> none  [the longest x7 31.8 us: matmul(): return jnp.dot(left, right, preferred_element_type=jnp.float32)]
    convert_element_type x3 -> x0, other arithmetic: 6.56 us -> none  [the longest x1 2.44 us: body(): (first * gate_dot * upper + silu_val * upper_dot).astype(jnp.bfloat16)]
    pallas_call x1, Pallas kernels: 9.41 us -> 13.8 us  [weight_products(): pl.pallas_call(products_kernel, grid=(width // tile,), in_specs=[pl.Block...]
where the time goes in v2:
time: 242 us; the launch traced here: 241 us
  Pallas kernels  239 us (99%)
    pallas_call x1, Pallas kernels, run(): pl.pallas_call(functools.partial(hvp_kernel, z, 1.0 / math.sqrt(TOKENS),...  225 us
    pallas_call x1, Pallas kernels, weight_products(): pl.pallas_call(products_kernel, grid=(width // tile,), in_specs=[pl.Block...  13.8 us

profile of v2, /device:TPU:0, one launch (start us, length us, event | category | flops | bytes accessed | tf_op | source)
XLA Modules:
  0.0 241.5 jit_solution(13010479321793615252)
XLA Ops:
  0.6 224.9 %shard_map.103 = (bf16[256,1024]{1,0:T(8,128)(2,1)}, bf16[256,3584]{1,0:T(8,128)(2,1)}, bf16[256,3584]{1,0:T(8,128)(2,1)}, bf16[2,256,1024]{2,1,0:T(8,128)(2,1)}...) custom-call(bf16[64,1024]{1,0:T(8,128)(2,1)} %refs_0_.1, bf16[64,1024]{1,0:T(8,128)(2,1)} %refs_1_.1, ...), custom_call_target="tpu_custom_call" | custom-call | flops 18790481920 | bytes 55050240 | tf_op jit(solution)/shard_map/pallas_call | solution.py:564
  225.6 2.1 copy.11
  227.7 13.8 %shard_map.104 = (bf16[1024,3584]{1,0:T(8,128)(2,1)}, bf16[1024,3584]{1,0:T(8,128)(2,1)}, bf16[3584,1024]{1,0:T(8,128)(2,1)}) custom-call(bf16[1024,256]{1,0:T(8,128)(2,1)} %bitcast.1, bf16[256,3584]{1,0:T(8,128)(2,1)} %get-tuple-element.10.gate, bf16[256,3584]{1,0:T(8,128)(2,1)} %get-tuple-element.11.upper, bf16[256,3584]{1,0:T(8,128)(2,1)} %get-tuple-element.12.hidden, ...), custom_call_target="tpu_custom_call" | custom-call | flops 7516192768 | bytes 29360128 | tf_op jit(solution)/shard_map/pallas_call | solution.py:617

commit v3 on v2

--- a/solution.py
+++ b/solution.py
@@ -9,7 +9,9 @@
 from jax.sharding import PartitionSpec as P
 
 TOKENS = 256
-CHUNKS = (512, 256, 128)
+CHUNKS = (256, 128)
+TILES = (896, 512, 256, 128)
+LAG_UP, LAG_MIDDLE, LAG_BACK = 2, 2, 3
 F32, BF16 = jnp.float32, jnp.bfloat16
 
 
@@ -72,8 +74,8 @@
 
 
 class Stream:
-    def __init__(self, sizes, na, nb):
-        self.z, self.na, self.nb = sizes, na, nb
+    def __init__(self, sizes, na, nb, lag):
+        self.z, self.na, self.nb, self.lag = sizes, na, nb, lag
 
     def scratch(self):
         z, na, nb = self.z, self.na, self.nb
@@ -81,7 +83,7 @@
         sem = pltpu.SemaphoreType.DMA
         pairs = [(n,), (2, n), (2, n), (n,), (2, n), (2, n), (n,), (2, n)]
         return [
-            pltpu.VMEM((na + nb, z.line, z.rows, c), F32),
+            pltpu.VMEM((na + nb, self.lag * z.line, z.rows, c), F32),
             pltpu.VMEM((n, na, 2, g, c), BF16),
             pltpu.VMEM((n, na, 2, g, c), BF16),
             pltpu.VMEM((2, n, na, g, c), BF16),
@@ -158,7 +160,7 @@
         n, part, a, b = z.items, self.part, self.a, self.b
         for d in (0, 1):
             p = self.place[d]
-            k, h = t - z.line - 1 - p, t - z.line - p
+            k, h = t - self.lag * (z.line + 1 + p), t - self.lag * (z.line + p)
             go = between(k, 0, n)
 
             @pl.when(both(go, p > 0))
@@ -186,13 +188,13 @@
             def _():
                 self.g_copy(d, k).wait_recv()
 
-        k = t - z.line
+        k = t - self.lag * z.line
 
         @pl.when(both(between(k, 0, n), self.at_end))
         def _():
             self.a_copy(self.end, k).wait_recv()
             self.f_copy(k).wait_recv()
-            slot, mine = lax.rem(k, z.line), self.group_of(self.end, side)
+            slot, mine = lax.rem(k, self.lag * z.line), self.group_of(self.end, side)
             sums = [part[i, slot, mine, :] + a[self.end, k, i].astype(F32) for i in range(na)]
             sums += [part[na + i, slot, mine, :] + self.f_in[k, i].astype(F32) for i in range(nb)]
             first, second = self.combine(k, sums)
@@ -204,12 +206,12 @@
 
         for d in (0, 1):
             p = self.place[d]
-            k = t - p
+            k = t - self.lag * p
 
             @pl.when(both(between(k, 0, n), between(p, 1, last)))
             def _():
                 self.b_copy(d, k).wait_recv()
-                slot, slab = lax.rem(k, z.line), span(d, 2 * z.group)
+                slot, slab = lax.rem(k, self.lag * z.line), span(d, 2 * z.group)
                 for i in range(nb):
                     b[d, k, i] = (part[na + i, slot, slab, :] + b[d, k, i].astype(F32)).astype(BF16)
                 self.b_copy(d, k).start()
@@ -217,7 +219,7 @@
             @pl.when(both(between(k, 0, n), p == last))
             def _():
                 self.b_copy(d, k).wait_recv()
-                slot = lax.rem(k, z.line)
+                slot = lax.rem(k, self.lag * z.line)
                 own, other = span(side, z.group), span(1 - side, z.group)
                 for i in range(nb):
                     self.f_out[k, i] = (
@@ -228,27 +230,27 @@
                 for i in range(nb):
                     part[na + i, slot, self.group_of(d, side), :] += b[d, k, i, own, :].astype(F32)
 
-        k = t - 1
+        k = t - self.lag
 
         @pl.when(between(k, 0, n))
         def _():
             self.y_copy(k).wait_recv()
             for i in range(na):
                 for e in (0, 1):
-                    part[i, lax.rem(k, z.line), self.group_of(e, side), :] += self.y_in[
+                    part[i, lax.rem(k, self.lag * z.line), self.group_of(e, side), :] += self.y_in[
                         k, i, e
                     ].astype(F32)
 
         for d in (0, 1):
             p = self.place[d]
-            k = t - 1 - p
+            k = t - self.lag * (1 + p)
 
             @pl.when(both(between(k, 0, n), between(p, 1, last)))
             def _():
                 self.a_copy(d, k).wait_recv()
                 for i in range(na):
                     a[d, k, i] = (
-                        part[i, lax.rem(k, z.line), self.group_of(d, side), :]
+                        part[i, lax.rem(k, self.lag * z.line), self.group_of(d, side), :]
                         + a[d, k, i].astype(F32)
                     ).astype(BF16)
                 self.a_copy(d, k).start()
@@ -256,7 +258,7 @@
             @pl.when(both(between(k, 0, n), p == 0))
             def _():
                 for i in range(na):
-                    a[d, k, i] = part[i, lax.rem(k, z.line), self.group_of(d, side), :].astype(BF16)
+                    a[d, k, i] = part[i, lax.rem(k, self.lag * z.line), self.group_of(d, side), :].astype(BF16)
                 self.a_copy(d, k).start()
 
     def late(self, t):
@@ -264,7 +266,7 @@
 
         @pl.when(between(t, 0, z.items))
         def _():
-            slot = lax.rem(t, z.line)
+            slot = lax.rem(t, self.lag * z.line)
             self.produce(t, self.part, slot)
             for i in range(na):
                 for e in (0, 1):
@@ -281,7 +283,7 @@
                 self.b_copy(d, t).start()
 
         if self.consume is not None:
-            k = t - 2 * z.line
+            k = t - 2 * self.lag * z.line
 
             @pl.when(between(k, 0, z.items))
             def _():
@@ -434,15 +436,20 @@
             x_copy(h, s).start()
         x_side(h).start()
         x_rows(h, me)[...] = tokens[h * z.own : (h + 1) * z.own, :]
-    for h in range(z.halves):
+
+    def x_relay(h):
         for s in hops:
             x_copy(h, s).wait_recv()
             x_pass(h, s).start()
-    for h in range(z.halves):
+
+    def x_take(h):
         x_side(h).wait_recv()
         for s in hops:
             x_pass(h, s).wait_recv()
 
+    x_relay(0)
+    x_take(0)
+
     def own_rows(index):
         return span(index, z.own)
 
@@ -465,8 +472,8 @@
         block = grad_rows(h, sources[s])
         return remote(block, block, m4, (h, s), "gy", other)
 
-    ready = z.steps - 1 + 2 * z.line
-    start_back = ready + 4
+    ready = z.steps - 1 + 2 * LAG_UP * z.line
+    start_back = ready + 3 * LAG_MIDDLE
 
     def middle_send(t):
         for h in range(z.halves):
@@ -482,7 +489,7 @@
         for h in range(z.halves):
             base = ready + h * z.steps
 
-            @pl.when(t == base + 1)
+            @pl.when(t == base + LAG_MIDDLE)
             def _():
                 m1_copy(h).wait_recv()
                 for i in (0, 1):
@@ -495,7 +502,7 @@
                         ).astype(BF16)
                     m2_copy(h, s).start()
 
-            @pl.when(t == base + 2)
+            @pl.when(t == base + 2 * LAG_MIDDLE)
             def _():
                 outs = [totals[h, i, own_rows(me), :] for i in (0, 1)]
                 for s in hops:
@@ -508,28 +515,38 @@
                     m3_copy(h, s).start()
                 m3_side(h).start()
 
-            @pl.when(t == base + 3)
+            @pl.when(t == base + 3 * LAG_MIDDLE)
             def _():
                 for s in hops:
                     m3_copy(h, s).wait_recv()
                     m4_copy(h, s).start()
 
-            @pl.when(t == base + 4)
+    def middle_take(t):
+        for h in range(z.halves):
+
+            @pl.when(t == ready + h * z.steps + 3 * LAG_MIDDLE)
             def _():
                 m3_side(h).wait_recv()
                 for s in hops:
                     m4_copy(h, s).wait_recv()
 
+    def x_later(t):
+        for h in range(1, z.halves):
+            pl.when(t == 1)(lambda: x_relay(h))
+            pl.when(t == 3)(lambda: x_take(h))
+
     def step(t, carry):
+        x_later(t)
         forward.early(t)
         middle(t)
         backward.early(t - start_back)
         forward.late(t)
         middle_send(t)
+        middle_take(t)
         backward.late(t - start_back)
         return carry
 
-    lax.fori_loop(0, start_back + z.items + 2 * z.line, step, 0)
+    lax.fori_loop(0, start_back + z.items + 2 * LAG_BACK * z.line, step, 0)
 
     for h in range(z.halves):
         for s in hops:
@@ -554,7 +571,7 @@
     z = Sizes(tokens, w_gate)
     model = w_down.shape[1]
     tall = z.halves * z.rows
-    forward, backward = Stream(z, 2, 2), Stream(z, 1, 1)
+    forward, backward = Stream(z, 2, 2, LAG_UP), Stream(z, 1, 1, LAG_BACK)
     vmem, any_spec = pl.BlockSpec(memory_space=pltpu.VMEM), pl.BlockSpec(memory_space=pl.ANY)
     sem = pltpu.SemaphoreType.DMA
     hops = max(z.pairs - 1, 1)
@@ -601,24 +618,24 @@
     )(tokens, target, w_gate, w_up, t_gate, t_up, w_down, t_down)
 
 
-def products_kernel(turned, gate, upper, hidden, hidden_dot, grads, out_gate, out_up, out_down):
-    out_gate[...] = matmul(turned[...], gate[...]).astype(BF16)
-    out_up[...] = matmul(turned[...], upper[...]).astype(BF16)
+def products_kernel(tokens, gate, upper, hidden, hidden_dot, grads, out_gate, out_up, out_down):
+    out_gate[...] = lead_dot(tokens[...], gate[...]).astype(BF16)
+    out_up[...] = lead_dot(tokens[...], upper[...]).astype(BF16)
     out_down[...] = (
         lead_dot(hidden_dot[...], grads[0]) + lead_dot(hidden[...], grads[1])
     ).astype(BF16)
 
 
-def weight_products(turned, gate, upper, hidden, hidden_dot, grads):
-    depth, rows = turned.shape
+def weight_products(tokens, gate, upper, hidden, hidden_dot, grads):
+    rows, depth = tokens.shape
     width, model = gate.shape[1], grads.shape[2]
-    tile = next(size for size in CHUNKS if width % size == 0)
+    tile = next(size for size in TILES if width % size == 0)
     strip = pl.BlockSpec((rows, tile), lambda i: (0, i))
     return pl.pallas_call(
         products_kernel,
         grid=(width // tile,),
         in_specs=[
-            pl.BlockSpec((depth, rows), lambda i: (0, 0)),
+            pl.BlockSpec((rows, depth), lambda i: (0, 0)),
             *[strip] * 4,
             pl.BlockSpec((2, rows, model), lambda i: (0, 0, 0)),
         ],
@@ -637,15 +654,14 @@
             bytes_accessed=2 * (2 * depth + model + 4 * rows) * width,
             transcendentals=0,
         ),
-    )(turned, gate, upper, hidden, hidden_dot, grads)
+    )(tokens, gate, upper, hidden, hidden_dot, grads)
 
 
 def body(tokens, target, w_gate, w_up, w_down, t_gate, t_up, t_down):
     x_full, hidden, hidden_dot, grads, gate_in, upper_in = run(
         tokens, target, w_gate, w_up, w_down, t_gate, t_up, t_down
     )
-    turned = lax.optimization_barrier(x_full.T)
-    return tuple(weight_products(turned, gate_in, upper_in, hidden, hidden_dot, grads))
+    return tuple(weight_products(x_full, gate_in, upper_in, hidden, hidden_dot, grads))
 
 
 def solution(mesh):

time: 242 us -> 220 us (0.909)
  Pallas kernels: 239 us -> 219 us
    pallas_call x1, Pallas kernels: 225 us -> 206 us  [run(): pl.pallas_call(functools.partial(hvp_kernel, z, 1.0 / math.sqrt(TOKENS),...]
where the time goes in v3:
time: 220 us; the launch traced here: 219 us
  Pallas kernels  219 us (100%)
    pallas_call x1, Pallas kernels, run(): pl.pallas_call(functools.partial(hvp_kernel, z, 1.0 / math.sqrt(TOKENS),...  206 us
    pallas_call x1, Pallas kernels, weight_products(): pl.pallas_call(products_kernel, grid=(width // tile,), in_specs=[pl.Block...  12.9 us

profile of v3, /device:TPU:0, one launch (start us, length us, event | category | flops | bytes accessed | tf_op | source)
XLA Modules:
  0.0 219.3 jit_solution(1230197530580655658)
XLA Ops:
  0.6 205.8 %shard_map.103 = (bf16[256,1024]{1,0:T(8,128)(2,1)}, bf16[256,3584]{1,0:T(8,128)(2,1)}, bf16[256,3584]{1,0:T(8,128)(2,1)}, bf16[2,256,1024]{2,1,0:T(8,128)(2,1)}...) custom-call(bf16[64,1024]{1,0:T(8,128)(2,1)} %refs_0_.1, bf16[64,1024]{1,0:T(8,128)(2,1)} %refs_1_.1, ...), custom_call_target="tpu_custom_call" | custom-call | flops 18790481920 | bytes 55050240 | tf_op jit(solution)/shard_map/pallas_call | solution.py:581
  206.4 12.9 %shard_map.104 = (bf16[1024,3584]{1,0:T(8,128)(2,1)}, bf16[1024,3584]{1,0:T(8,128)(2,1)}, bf16[3584,1024]{1,0:T(8,128)(2,1)}) custom-call(bf16[256,1024]{1,0:T(8,128)(2,1)} %get-tuple-element.9.tokens, bf16[256,3584]{1,0:T(8,128)(2,1)} %get-tuple-element.10.gate, bf16[256,3584]{1,0:T(8,128)(2,1)} %get-tuple-element.11.upper, ...), custom_call_target="tpu_custom_call" | custom-call | flops 7516192768 | bytes 29360128 | tf_op jit(solution)/shard_map/pallas_call | solution.py:634

commit v4 on v3

--- a/solution.py
+++ b/solution.py
@@ -9,9 +9,10 @@
 from jax.sharding import PartitionSpec as P
 
 TOKENS = 256
-CHUNKS = (256, 128)
+CHUNKS = (512, 256, 128)
 TILES = (896, 512, 256, 128)
-LAG_UP, LAG_MIDDLE, LAG_BACK = 2, 2, 3
+LAG_UP, LAG_BACK = 2, 3
+MIDDLE = (1, 3, 5)
 F32, BF16 = jnp.float32, jnp.bfloat16
 
 
@@ -64,7 +65,7 @@
         self.pairs = self.gy // 2
         own, self.depth = tokens.shape
         self.width = w_gate.shape[1]
-        self.halves = 2 if own % 32 == 0 else 1
+        self.halves = next(parts for parts in (4, 2, 1) if own % (16 * parts) == 0)
         self.own = own // self.halves
         self.rows = self.own * self.gy
         self.group = self.rows // 4
@@ -335,13 +336,15 @@
 
 def hvp_kernel(z, scale, forward, backward, *refs):
     tokens, target, w_gate, w_up, t_gate, t_up, w_down, t_down = refs[:8]
-    x_full, hid, hid_dot, grads, gate_in, upper_in = refs[8:14]
+    results = refs[8:14]
     count = len(forward.scratch())
     f_refs, b_refs, rest = refs[14 : 14 + count], refs[14 + count : 14 + 2 * count], refs[14 + 2 * count :]
     up_slots, up_sems, down_slots, down_sems, back_slots, back_sems = rest[:6]
     totals, saved, m1_out, m1_in, m2_out, m2_in = rest[6:12]
     sems = [(rest[12 + 2 * i], rest[13 + 2 * i]) for i in range(8)]
     x1, x2, x3, m1, m2, m3, m3p, m4 = sems
+    held, whole_sems, item_sems = rest[28:34], rest[34], rest[35]
+    x_full, hid, hid_dot, grads, gate_in, upper_in = held
 
     me = lax.axis_index("gy")
     core, pair = lax.rem(me, 2), lax.div(me, 2)
@@ -397,8 +400,21 @@
             (back_dot * silu_val + back * first * gate_dot).astype(BF16),
         )
 
+    def whole_out(i):
+        return pltpu.make_async_copy(held[i], results[i], whole_sems.at[i])
+
+    def item_out(i, k):
+        block = (half_rows(k), span(lax.rem(k, z.steps), z.chunk))
+        return pltpu.make_async_copy(
+            held[4 + i].at[block], results[4 + i].at[block], item_sems.at[i, k]
+        )
+
+    def consume_back(k):
+        for i in (0, 1):
+            item_out(i, k).start()
+
     forward.bind(f_refs, hid, hid_dot, produce_up, combine_up, consume_up)
-    backward.bind(b_refs, gate_in, upper_in, produce_back, combine_back, None)
+    backward.bind(b_refs, gate_in, upper_in, produce_back, combine_back, consume_back)
 
     barrier = pltpu.get_barrier_semaphore()
 
@@ -473,7 +489,7 @@
         return remote(block, block, m4, (h, s), "gy", other)
 
     ready = z.steps - 1 + 2 * LAG_UP * z.line
-    start_back = ready + 3 * LAG_MIDDLE
+    start_back = ready + MIDDLE[2]
 
     def middle_send(t):
         for h in range(z.halves):
@@ -484,12 +500,15 @@
                     for g in range(z.pairs):
                         m1_out[h, i, g] = totals[h, i, own_rows(g * 2 + 1 - core), :].astype(BF16)
                 m1_copy(h).start()
+                if h == z.halves - 1:
+                    whole_out(1).start()
+                    whole_out(2).start()
 
     def middle(t):
         for h in range(z.halves):
             base = ready + h * z.steps
 
-            @pl.when(t == base + LAG_MIDDLE)
+            @pl.when(t == base + MIDDLE[0])
             def _():
                 m1_copy(h).wait_recv()
                 for i in (0, 1):
@@ -502,7 +521,7 @@
                         ).astype(BF16)
                     m2_copy(h, s).start()
 
-            @pl.when(t == base + 2 * LAG_MIDDLE)
+            @pl.when(t == base + MIDDLE[1])
             def _():
                 outs = [totals[h, i, own_rows(me), :] for i in (0, 1)]
                 for s in hops:
@@ -515,7 +534,7 @@
                     m3_copy(h, s).start()
                 m3_side(h).start()
 
-            @pl.when(t == base + 3 * LAG_MIDDLE)
+            @pl.when(t == base + MIDDLE[2])
             def _():
                 for s in hops:
                     m3_copy(h, s).wait_recv()
@@ -524,16 +543,19 @@
     def middle_take(t):
         for h in range(z.halves):
 
-            @pl.when(t == ready + h * z.steps + 3 * LAG_MIDDLE)
+            @pl.when(t == ready + h * z.steps + MIDDLE[2])
             def _():
                 m3_side(h).wait_recv()
                 for s in hops:
                     m4_copy(h, s).wait_recv()
+                if h == z.halves - 1:
+                    whole_out(3).start()
 
     def x_later(t):
         for h in range(1, z.halves):
             pl.when(t == 1)(lambda: x_relay(h))
             pl.when(t == 3)(lambda: x_take(h))
+        pl.when(t == 4)(lambda: whole_out(0).start())
 
     def step(t, carry):
         x_later(t)
@@ -562,9 +584,13 @@
     def settle(k, carry):
         forward.settle(k)
         backward.settle(k)
+        for i in (0, 1):
+            item_out(i, k).wait()
         return carry
 
     lax.fori_loop(0, z.items, settle, 0)
+    for i in range(4):
+        whole_out(i).wait()
 
 
 def run(tokens, target, w_gate, w_up, w_down, t_gate, t_up, t_down):
@@ -578,18 +604,19 @@
     wide = jax.ShapeDtypeStruct((tall, z.width), BF16)
     marks = [(z.halves, hops), (z.halves,), (z.halves, hops), (z.halves,), (z.halves, hops),
              (z.halves, hops), (z.halves,), (z.halves, hops)]
+    outs = [
+        jax.ShapeDtypeStruct((tall, z.depth), BF16),
+        wide,
+        wide,
+        jax.ShapeDtypeStruct((2, tall, model), BF16),
+        wide,
+        wide,
+    ]
     return pl.pallas_call(
         functools.partial(hvp_kernel, z, 1.0 / math.sqrt(TOKENS), forward, backward),
-        out_shape=[
-            jax.ShapeDtypeStruct((tall, z.depth), BF16),
-            wide,
-            wide,
-            jax.ShapeDtypeStruct((2, tall, model), BF16),
-            wide,
-            wide,
-        ],
+        out_shape=outs,
         in_specs=[vmem] * 2 + [any_spec] * 6,
-        out_specs=[vmem] * 6,
+        out_specs=[any_spec] * 6,
         scratch_shapes=[
             *forward.scratch(),
             *backward.scratch(),
@@ -606,6 +633,9 @@
             pltpu.VMEM((z.halves, hops, 2, z.own, model), BF16),
             pltpu.VMEM((z.halves, hops, 2, z.own, model), BF16),
             *[sem(shape) for shape in marks for _ in range(2)],
+            *[pltpu.VMEM(out.shape, out.dtype) for out in outs],
+            sem((4,)),
+            sem((2, z.items)),
         ],
         compiler_params=pltpu.CompilerParams(
             collective_id=0, has_side_effects=True, vmem_limit_bytes=67043328

time: 220 us -> 213 us (0.968)
  Pallas kernels: 219 us -> 212 us
    pallas_call x1, Pallas kernels: 206 us -> 199 us  [run(): pl.pallas_call(functools.partial(hvp_kernel, z, 1.0 / math.sqrt(TOKENS),...]
where the time goes in v4:
time: 213 us; the launch traced here: 212 us
  Pallas kernels  212 us (100%)
    pallas_call x1, Pallas kernels, run(): pl.pallas_call(functools.partial(hvp_kernel, z, 1.0 / math.sqrt(TOKENS),...  199 us
    pallas_call x1, Pallas kernels, weight_products(): pl.pallas_call(products_kernel, grid=(width // tile,), in_specs=[pl.Block...  12.9 us

profile of v4, /device:TPU:0, one launch (start us, length us, event | category | flops | bytes accessed | tf_op | source)
XLA Modules:
  0.0 212.4 jit_solution(5347367129470913135)
XLA Ops:
  0.6 198.8 %shard_map.103 = (bf16[256,1024]{1,0:T(8,128)(2,1)}, bf16[256,3584]{1,0:T(8,128)(2,1)}, bf16[256,3584]{1,0:T(8,128)(2,1)}, bf16[2,256,1024]{2,1,0:T(8,128)(2,1)}...) custom-call(bf16[64,1024]{1,0:T(8,128)(2,1)} %refs_0_.1, bf16[64,1024]{1,0:T(8,128)(2,1)} %refs_1_.1, ...), custom_call_target="tpu_custom_call" | custom-call | flops 18790481920 | bytes 55050240 | tf_op jit(solution)/shard_map/pallas_call | solution.py:615
  199.5 12.9 %shard_map.104 = (bf16[1024,3584]{1,0:T(8,128)(2,1)}, bf16[1024,3584]{1,0:T(8,128)(2,1)}, bf16[3584,1024]{1,0:T(8,128)(2,1)}) custom-call(bf16[256,1024]{1,0:T(8,128)(2,1)} %get-tuple-element.9.tokens, bf16[256,3584]{1,0:T(8,128)(2,1)} %get-tuple-element.10.gate, bf16[256,3584]{1,0:T(8,128)(2,1)} %get-tuple-element.11.upper, ...), custom_call_target="tpu_custom_call" | custom-call | flops 7516192768 | bytes 29360128 | tf_op jit(solution)/shard_map/pallas_call | solution.py:664

commit v5 on v4

--- a/solution.py
+++ b/solution.py
@@ -380,14 +380,16 @@
         weights = down.take(k)
         half, columns = lax.div(k, z.steps), span(lax.rem(k, z.steps), z.chunk)
         hidden, hidden_dot = hid[half_rows(k), columns], hid_dot[half_rows(k), columns]
-        totals[half, 0] += matmul(hidden, weights[0])
-        totals[half, 1] += matmul(hidden_dot, weights[0]) + matmul(hidden, weights[1])
+        joint = matmul(jnp.concatenate([hidden, hidden_dot], axis=0), weights[0])
+        totals[half, 0] += joint[: z.rows]
+        totals[half, 1] += joint[z.rows :] + matmul(hidden, weights[1])
 
     def produce_back(k, part, slot):
         weights = again.take(k)
         grad, grad_dot = grads[0, half_rows(k), :], grads[1, half_rows(k), :]
-        part[0, slot] = tail_dot(grad, weights[0])
-        part[1, slot] = tail_dot(grad_dot, weights[0]) + tail_dot(grad, weights[1])
+        joint = tail_dot(jnp.concatenate([grad, grad_dot], axis=0), weights[0])
+        part[0, slot] = joint[: z.rows]
+        part[1, slot] = joint[z.rows :] + tail_dot(grad, weights[1])
 
     def combine_back(k, sums):
         back, back_dot = sums

time: 213 us -> 208 us (0.977)
  Pallas kernels: 212 us -> 207 us
    pallas_call x1, Pallas kernels: 199 us -> 194 us  [run(): pl.pallas_call(functools.partial(hvp_kernel, z, 1.0 / math.sqrt(TOKENS),...]
where the time goes in v5:
time: 208 us
  Pallas kernels  207 us (100%)
    pallas_call x1, Pallas kernels, run(): pl.pallas_call(functools.partial(hvp_kernel, z, 1.0 / math.sqrt(TOKENS),...  194 us
    pallas_call x1, Pallas kernels, weight_products(): pl.pallas_call(products_kernel, grid=(width // tile,), in_specs=[pl.Block...  12.9 us

profile of v5, /device:TPU:0, one launch (start us, length us, event | category | flops | bytes accessed | tf_op | source)
XLA Modules:
  0.0 207.7 jit_solution(15761417400819154596)
XLA Ops:
  0.6 194.1 %shard_map.103 = (bf16[256,1024]{1,0:T(8,128)(2,1)}, bf16[256,3584]{1,0:T(8,128)(2,1)}, bf16[256,3584]{1,0:T(8,128)(2,1)}, bf16[2,256,1024]{2,1,0:T(8,128)(2,1)}...) custom-call(bf16[64,1024]{1,0:T(8,128)(2,1)} %refs_0_.1, bf16[64,1024]{1,0:T(8,128)(2,1)} %refs_1_.1, ...), custom_call_target="tpu_custom_call" | custom-call | flops 18790481920 | bytes 55050240 | tf_op jit(solution)/shard_map/pallas_call | solution.py:617
  194.7 12.9 %shard_map.104 = (bf16[1024,3584]{1,0:T(8,128)(2,1)}, bf16[1024,3584]{1,0:T(8,128)(2,1)}, bf16[3584,1024]{1,0:T(8,128)(2,1)}) custom-call(bf16[256,1024]{1,0:T(8,128)(2,1)} %get-tuple-element.9.tokens, bf16[256,3584]{1,0:T(8,128)(2,1)} %get-tuple-element.10.gate, bf16[256,3584]{1,0:T(8,128)(2,1)} %get-tuple-element.11.upper, ...), custom_call_target="tpu_custom_call" | custom-call | flops 7516192768 | bytes 29360128 | tf_op jit(solution)/shard_map/pallas_call | solution.py:666
